TPU v7x, 32 devices: a whole 2x2x4 slice. The times are simulated.
32 devices in a mesh: gx: 4 (over z), gy: 8 (over y, x, core).
Axes of the slice: x: 2, y: 2, z: 4, core: 2. Of those that a mesh axis runs over, the one named last changes fastest.
Arguments:
- atm_members: float32 [4, 8, 80, 12, 128], P('gx', 'gy'), may hold values from -6 to 6
- ocean_members: bfloat16 [4, 8, 80, 1024], P('gx', 'gy'), may hold values from -6 to 6
- remap_weights: bfloat16 [4, 8, 4, 1024, 128], P('gx', 'gy'), may hold values from -0.09375 to 0.09375
- pair_src: int32 [4, 8, 4], P('gx', 'gy'), may hold values from 0 to 31, as said below
- obs_cell: int32 [4, 8, 64], P('gx', 'gy'), may hold values from 0 to 127
- obs_value: float32 [4, 8, 64], P('gx', 'gy'), may hold values from -8 to 8
- obs_error: float32 [4, 8, 64], P('gx', 'gy'), may hold values from 2 to 16
- obs_live: int32 [4, 8, 64], P('gx', 'gy'), may hold values from 0 to 1, as said below
- obs_order: int32 [4, 8, 64], P('gx', 'gy'), may hold values from 0 to 63, each once within a row
Outputs:
- post_mean: float32 [4, 8, 13, 128], P('gx', 'gy')
- post_anom: float32 [4, 8, 80, 13, 128], P('gx', 'gy')
Inputs may be any that keep to these rules, and one draw needn't show every extreme that they name: `pair_src`: for atmosphere tile (i, j) the 4 numbers are distinct, each a * 8 + b with |a - i| <= 1 and |b - j| <= 1. `obs_live`: the live slots of a tile are its first ones, between 8 and 64 of them; some tile has all slots live. `obs_order`: each tile's last dimension is a permutation of its slots.
All inputs are finite; a program needn't handle non-finite values.
Results may differ from a plain program's by a relative error of at most 0.0003.
Values may be sent and summed in bfloat16 or wider, within the bound.
A program may use at most 64 MiB of HBM per device.

v0:
```python
import functools

import jax
import jax.numpy as jnp
import numpy as np
from jax import lax
from jax.experimental import pallas as pl
from jax.experimental.pallas import tpu as pltpu
from jax.sharding import PartitionSpec as P

AX = 8
AY = 16
OB = 32
NB = 2
RAD = 2
CODE = 64
LIMIT = 65400 * 1024

MESH = pl.DeviceIdType.MESH
OFFS = [(dx, dy) for dx in (-1, 0, 1) for dy in (-1, 0, 1)]
OTHERS = [i for i in range(9) if i != 4]


def taper_of(dx, dy):
    return max(1.0 - (dx * dx + dy * dy) / float(RAD * RAD), 0.0) ** 2


@functools.lru_cache
def tables():
    cells = AX * AY
    own = [(c // AY, c % AY) for c in range(cells)]
    halo = [
        (x, y)
        for x in range(-RAD, AX + RAD)
        for y in range(-RAD, AY + RAD)
        if not (0 <= x < AX and 0 <= y < AY)
    ]
    lanes = own + halo
    where = {xy: n for n, xy in enumerate(lanes)}
    code = np.full((8, 2 * cells), -1.0, np.float32)
    for n, (x, y) in enumerate(lanes):
        code[:, n] = (x + AX) * CODE + (y + AY)
    move = np.zeros((2 * cells, 2, 8, cells), np.float32)
    for n, (x, y) in enumerate(lanes):
        for d, i in enumerate(OTHERS):
            dx, dy = OFFS[i]
            src = where.get((x + dx, y + dy))
            if src is not None:
                move[src, n // cells, d, n % cells] = 1.0
    pick = np.zeros((8, cells, cells), np.float32)
    for n, (x, y) in enumerate(halo):
        i = (x // AX + 1) * 3 + (y // AY + 1)
        pick[OTHERS.index(i), (x % AX) * AY + (y % AY), n] = 1.0
    return code, move.reshape(2 * cells, 16 * cells), pick.reshape(8 * cells, cells)


def split_rows(block):
    high = block.astype(jnp.bfloat16).astype(jnp.float32)
    return jnp.concatenate([high, block - high], axis=0).astype(jnp.bfloat16)


def exchange_kernel(
    src_ref, order_ref, cell_ref, live_ref, value_ref, error_ref, ocean_ref, weights_ref, atm_ref,
    tiles_ref, metat_ref, fields_ref, fmean_ref,
    ocn, wts, meta, src, order_in, cell_in, live_in, value_in, error_in,
    own, blank, metat, held, fmean,
    local_sem, send_sem, recv_sem, out_sem,
):
    gx, gy = lax.axis_index("gx"), lax.axis_index("gy")
    nx, ny = lax.axis_size("gx"), lax.axis_size("gy")
    members = tiles_ref.shape[1]
    fields = atm_ref.shape[0]
    slots = order_in.shape[1]

    def has_x(dx):
        return (gx + dx >= 0) & (gx + dx < nx)

    def has_y(dy):
        return (gy + dy >= 0) & (gy + dy < ny)

    def there(i):
        return has_x(OFFS[i][0]) & has_y(OFFS[i][1])

    pairs = (
        (ocean_ref, ocn.at[4]), (order_ref, order_in), (cell_ref, cell_in), (live_ref, live_in),
        (value_ref, value_in), (error_ref, error_in), (src_ref, src), (weights_ref, wts),
        (atm_ref, held),
    )
    staged = [pltpu.make_async_copy(x, y, local_sem.at[n]) for n, (x, y) in enumerate(pairs)]
    for copy in staged:
        copy.start()

    blank[...] = jnp.zeros(blank.shape, jnp.float32)
    barrier = pltpu.get_barrier_semaphore()
    for i in OTHERS:
        dx, dy = OFFS[i]

        @pl.when(there(i))
        def _():
            pl.semaphore_signal(barrier, inc=1, device_id=(gx + dx, gy + dy), device_id_type=MESH)

    for i in OTHERS:

        @pl.when(jnp.logical_not(there(i)))
        def _():
            pltpu.make_async_copy(blank, tiles_ref.at[i], out_sem.at[i]).start()
            meta[i] = jnp.zeros(meta.shape[1:], jnp.float32)

    for n in range(9, meta.shape[0]):
        meta[n] = jnp.zeros(meta.shape[1:], jnp.float32)

    for copy in staged[1:6]:
        copy.wait()
    cell = cell_in[...]
    spot = ((cell // AY) * CODE + cell % AY).astype(jnp.float32)
    rows = jnp.concatenate(
        [
            spot, value_in[...], error_in[...], live_in[...].astype(jnp.float32),
            jnp.zeros((4, slots), jnp.float32),
        ],
        axis=0,
    )
    slot = lax.broadcasted_iota(jnp.int32, (slots, slots), 0)
    perm = jnp.where(order_in[...] == slot, 1.0, 0.0)
    rows = jnp.dot(rows, perm, precision=lax.Precision.HIGHEST, preferred_element_type=jnp.float32)
    meta[4] = jnp.concatenate([rows, jnp.zeros((8, meta.shape[2] - slots), jnp.float32)], axis=1)

    staged[0].wait()
    across = 1 + has_x(-1).astype(jnp.int32) + has_x(1).astype(jnp.int32)
    along = 1 + has_y(-1).astype(jnp.int32) + has_y(1).astype(jnp.int32)
    pl.semaphore_wait(barrier, across * along - 1)

    outer = lax.rem(gy, 2) * 2 - 1

    first = (members // 2 + 15) // 16 * 16
    parts = ((0, 0, first), (3, first, members - first))

    def ocean(part, source, target, n, dx, dy):
        kind, low, size = part
        return pltpu.make_async_remote_copy(
            src_ref=ocn.at[source, pl.ds(low, size)],
            dst_ref=ocn.at[target, pl.ds(low, size)],
            send_sem=send_sem.at[kind, n],
            recv_sem=recv_sem.at[kind, target],
            device_id=(gx + dx, gy + dy),
            device_id_type=MESH,
        )

    def arrive(part, at, dx, dy):
        ocean(part, at, at, 4, dx, dy).wait_recv()

    firsts = [
        (cond, ocean(part, 4, target, n, dx, dy))
        for part in parts
        for cond, target, n, dx, dy in (
            (has_y(outer), 4 - outer, 1, 0, outer),
            (has_x(-1), 7, 2, -1, 0),
            (has_x(1), 1, 3, 1, 0),
            (has_y(-outer), 4 + outer, 0, 0, -outer),
        )
    ]
    relays = [
        (has_y(outer) & has_x(dx), ocean(part, 4 + outer, 4 - 3 * dx + outer, n, dx, 0))
        for part in parts
        for dx, n in ((-1, 5), (1, 6))
    ]
    hands = [
        (
            part, dx, has_x(dx) & has_y(-outer),
            ocean(part, 4 + 3 * dx, 4 + 3 * dx + outer, n, 0, -outer),
        )
        for part in parts
        for dx, n in ((-1, 7), (1, 8))
    ]

    def begin(cond, copy):
        @pl.when(cond)
        def _():
            copy.start()

    for cond, copy in firsts:
        begin(cond, copy)

    def remote(buf, kind, i):
        dx, dy = OFFS[i]
        return pltpu.make_async_remote_copy(
            src_ref=buf.at[4],
            dst_ref=buf.at[8 - i],
            send_sem=send_sem.at[kind, i],
            recv_sem=recv_sem.at[kind, 8 - i],
            device_id=(gx + dx, gy + dy),
            device_id_type=MESH,
        )

    def column(i):
        dx, dy = OFFS[i]
        return pltpu.make_async_remote_copy(
            src_ref=own,
            dst_ref=tiles_ref.at[8 - i],
            send_sem=send_sem.at[2, i],
            recv_sem=recv_sem.at[2, 8 - i],
            device_id=(gx + dx, gy + dy),
            device_id_type=MESH,
        )

    def send(buf, kind):
        for i in OTHERS:

            @pl.when(there(i))
            def _():
                remote(buf, kind, i).start()

    def receive(buf, kind):
        for i in OTHERS:

            @pl.when(there(i))
            def _():
                remote(buf, kind, 8 - i).wait_recv()

    def settle(buf, kind):
        for i in OTHERS:

            @pl.when(there(i))
            def _():
                remote(buf, kind, i).wait_send()

    send(meta, 1)

    staged[8].wait()
    for v in range(fields):
        block = held[v]
        mean = jnp.sum(block, axis=0, keepdims=True) / members
        fmean[v : v + 1, :] = mean
        held[v] = block - mean
    results = [
        pltpu.make_async_copy(held, fields_ref, local_sem.at[9]),
        pltpu.make_async_copy(fmean, fmean_ref, local_sem.at[10]),
        pltpu.make_async_copy(metat, metat_ref, local_sem.at[11]),
        pltpu.make_async_copy(own, tiles_ref.at[4], out_sem.at[4]),
    ]
    results[0].start()
    results[1].start()

    for at, part in enumerate(parts):

        @pl.when(has_y(outer))
        def _():
            arrive(part, 4 + outer, 0, outer)

        for cond, copy in relays[2 * at : 2 * at + 2]:
            begin(cond, copy)
    for part, dx, cond, copy in hands:

        @pl.when(has_x(dx))
        def _():
            arrive(part, 4 + 3 * dx, dx, 0)

        begin(cond, copy)

    receive(meta, 1)
    flat = meta[...].reshape(meta.shape[0] * meta.shape[1], meta.shape[2])
    metat[...] = flat.T
    results[2].start()
    staged[6].wait()
    staged[7].wait()

    for part in parts:

        @pl.when(has_y(-outer))
        def _():
            arrive(part, 4 - outer, 0, -outer)

        for dx in (-1, 1):
            for dy in (outer, -outer):

                @pl.when(has_x(dx) & has_y(dy))
                def _():
                    arrive(part, 4 + 3 * dx + dy, dx, 0)

    total = jnp.zeros(tiles_ref.shape[1:], jnp.float32)
    for k in range(wts.shape[0]):
        source = src[0, k]
        position = (source // ny - gx + 1) * 3 + (source % ny - gy + 1)
        position = jnp.clip(position, 0, 8)
        total += jnp.dot(ocn[position], wts[k], preferred_element_type=jnp.float32)
    own[...] = total
    for i in OTHERS:

        @pl.when(there(i))
        def _():
            column(i).start()

    results[3].start()
    for cond, copy in firsts + relays + [hand[2:] for hand in hands]:

        @pl.when(cond)
        def _():
            copy.wait_send()

    settle(meta, 1)
    for copy in results:
        copy.wait()
    for i in OTHERS:

        @pl.when(jnp.logical_not(there(i)))
        def _():
            pltpu.make_async_copy(blank, tiles_ref.at[i], out_sem.at[i]).wait()

        @pl.when(there(i))
        def _():
            column(i).wait_send()
            column(8 - i).wait_recv()


def analysis_kernel(
    tiles_in, metat_in, fields_in, fmean_in, code_in, move_in, pick_in,
    mean_ref, anom_ref,
    tiles_ref, metat_ref, fmean_ref, code_ref, move_ref, pick_ref, held, shifted, local_sem, out_sem,
):
    fields, members, cells = fields_in.shape
    pairs = (
        (tiles_in, tiles_ref), (metat_in, metat_ref), (fmean_in, fmean_ref),
        (fields_in, held.at[0:fields]), (pick_in, pick_ref), (code_in, code_ref),
        (move_in, move_ref),
    )
    staged = [pltpu.make_async_copy(x, y, local_sem.at[n]) for n, (x, y) in enumerate(pairs)]
    for n in (0, 4, 1, 5, 6, 2, 3):
        staged[n].start()
    staged[0].wait()
    staged[4].wait()

    scale = 1.0 / (members - 1)
    beside = split_rows(jnp.concatenate([tiles_ref[i] for i in OTHERS], axis=1))
    halo = jnp.dot(beside, pick_ref[...], preferred_element_type=jnp.float32)
    grid = jnp.concatenate([tiles_ref[4], halo[:members] + halo[members:]], axis=1)
    gmean = jnp.sum(grid, axis=0, keepdims=True) / members
    grid = grid - gmean
    staged[1].wait()
    staged[5].wait()
    code = code_ref[0:1, :]

    for b in range(NB):
        last = b == NB - 1
        variance = jnp.sum(grid * grid, axis=0, keepdims=True) / (members - 1)
        gains = jnp.zeros((OB, 2 * cells), jnp.float32)
        sums = jnp.zeros((OB, 2 * cells), jnp.float32)
        weights = jnp.zeros((OB, 2 * cells), jnp.float32)
        for i in range(9):
            dx, dy = OFFS[i]
            column = metat_ref[b * OB : (b + 1) * OB, 8 * i : 8 * i + 4]
            spot = column[:, 0:1] + float((AX * dx + AX) * CODE + AY * dy + AY)
            error = column[:, 2:3]
            live = column[:, 3:4]
            denom = variance + (error + (1.0 - live))
            weighting = live / denom
            damping = 1.0 / (1.0 + jnp.sqrt(error / denom))
            hit = spot == code
            weighting = jnp.where(hit, weighting, 0.0)
            weights = weights + weighting
            gains = gains + weighting * damping
            sums = sums + weighting * column[:, 1:2]
        alpha = jnp.sum(gains, axis=0, keepdims=True)
        beta = jnp.sum(sums, axis=0, keepdims=True) - gmean * jnp.sum(weights, axis=0, keepdims=True)
        extra = jnp.concatenate([alpha, beta, jnp.zeros((6, 2 * cells), jnp.float32)], axis=0)
        if b == 0:
            staged[6].wait()
        left = split_rows(jnp.concatenate([grid, extra], axis=0))
        width = (8 if last else 16) * cells
        moved = jnp.dot(left, move_ref[:, :width], preferred_element_type=jnp.float32)
        rows = members + 8
        shifted[:, :width] = moved[:rows] + moved[rows:]

        def step(block, part, center, alpha, beta):
            total = jnp.zeros_like(block)
            mean = jnp.zeros((1, cells), jnp.float32)
            for d in range(9):
                if d == 8:
                    source, a, m = center, alpha * scale, beta * scale
                else:
                    dx, dy = OFFS[OTHERS[d]]
                    weight = scale * taper_of(dx, dy)
                    at = (part * 8 + d) * cells
                    source = shifted[:members, at : at + cells]
                    a = shifted[members : members + 1, at : at + cells] * weight
                    m = shifted[members + 1 : members + 2, at : at + cells] * weight
                cov = jnp.sum(block * source, axis=0, keepdims=True)
                mean = mean + cov * m
                total = total + source * (cov * a)
            return block - total, mean

        own = grid[:, :cells]
        held[fields] = own
        if b == 0:
            staged[2].wait()
            staged[3].wait()
        own_args = (alpha[:, :cells], beta[:, :cells])

        def one_field(v, carry, own_args=own_args, last=last, b=b, step=step):
            block, mean = step(held[v], 0, held[fields], *own_args)
            held[v] = block
            before = fmean_ref[pl.ds(v, 1), :] if b == 0 else mean_ref[v]
            mean_ref[v] = before + mean
            if last:
                pltpu.make_async_copy(held.at[v], anom_ref.at[v], out_sem.at[v]).start()
            return carry

        lax.fori_loop(0, fields, one_field, 0)
        block, mean = step(own, 0, own, *own_args)
        if last:
            held[fields] = block
            mean_ref[fields] = gmean[:, :cells] + mean
            pltpu.make_async_copy(
                held.at[fields], anom_ref.at[fields], out_sem.at[fields]
            ).start()
            for v in range(fields + 1):
                pltpu.make_async_copy(held.at[v], anom_ref.at[v], out_sem.at[v]).wait()
        else:
            outer = grid[:, cells:]
            far, far_mean = step(outer, 1, outer, alpha[:, cells:], beta[:, cells:])
            grid = jnp.concatenate([block, far], axis=1)
            gmean = gmean + jnp.concatenate([mean, far_mean], axis=1)


def local(
    atm_members, ocean_members, remap_weights, pair_src, obs_cell, obs_value, obs_error,
    obs_live, obs_order,
):
    members, fields, cells = atm_members.shape[2:]
    slots = obs_cell.shape[2]
    sources, depth = remap_weights.shape[2:4]
    vmem = pl.BlockSpec(memory_space=pltpu.VMEM)
    anywhere = pl.BlockSpec(memory_space=pl.ANY)
    code, move, pick = tables()
    results = (
        jax.ShapeDtypeStruct((9, members, cells), jnp.float32),
        jax.ShapeDtypeStruct((128, 128), jnp.float32),
        jax.ShapeDtypeStruct((fields, members, cells), jnp.float32),
        jax.ShapeDtypeStruct((fields, cells), jnp.float32),
    )
    state = pl.pallas_call(
        exchange_kernel,
        out_shape=results,
        in_specs=[anywhere] * 9,
        out_specs=(anywhere,) * 4,
        scratch_shapes=[
            pltpu.VMEM((9, members, depth), jnp.bfloat16),
            pltpu.VMEM((sources, depth, cells), jnp.bfloat16),
            pltpu.VMEM((16, 8, 128), jnp.float32),
            pltpu.SMEM((1, sources), jnp.int32),
            pltpu.VMEM((1, slots), jnp.int32),
            pltpu.VMEM((1, slots), jnp.int32),
            pltpu.VMEM((1, slots), jnp.int32),
            pltpu.VMEM((1, slots), jnp.float32),
            pltpu.VMEM((1, slots), jnp.float32),
            pltpu.VMEM((members, cells), jnp.float32),
            pltpu.VMEM((members, cells), jnp.float32),
            pltpu.VMEM((128, 128), jnp.float32),
            pltpu.VMEM((fields, members, cells), jnp.float32),
            pltpu.VMEM((fields, cells), jnp.float32),
            pltpu.SemaphoreType.DMA((12,)),
            pltpu.SemaphoreType.DMA((4, 9)),
            pltpu.SemaphoreType.DMA((4, 9)),
            pltpu.SemaphoreType.DMA((9,)),
        ],
        compiler_params=pltpu.CompilerParams(
            collective_id=0, has_side_effects=True, vmem_limit_bytes=LIMIT
        ),
        name="exchange",
    )(
        pair_src[0], obs_order[0], obs_cell[0], obs_live[0], obs_value[0], obs_error[0],
        ocean_members[0, 0], remap_weights[0, 0], jnp.transpose(atm_members[0, 0], (1, 0, 2)),
    )
    post_mean, post_anom = pl.pallas_call(
        analysis_kernel,
        out_shape=(
            jax.ShapeDtypeStruct((fields + 1, 1, cells), jnp.float32),
            jax.ShapeDtypeStruct((fields + 1, members, cells), jnp.float32),
        ),
        in_specs=[anywhere] * 7,
        out_specs=(vmem, anywhere),
        scratch_shapes=[
            *(pltpu.VMEM(r.shape, jnp.float32) for r in (results[0], results[1], results[3])),
            pltpu.VMEM(code.shape, jnp.float32),
            pltpu.VMEM(move.shape, jnp.bfloat16),
            pltpu.VMEM(pick.shape, jnp.bfloat16),
            pltpu.VMEM((fields + 1, members, cells), jnp.float32),
            pltpu.VMEM((members + 8, 16 * cells), jnp.float32),
            pltpu.SemaphoreType.DMA((7,)),
            pltpu.SemaphoreType.DMA((fields + 1,)),
        ],
        compiler_params=pltpu.CompilerParams(vmem_limit_bytes=LIMIT),
        name="analysis",
    )(*state, jnp.asarray(code), jnp.asarray(move, jnp.bfloat16), jnp.asarray(pick, jnp.bfloat16))
    return (post_mean.reshape(1, 1, fields + 1, cells), jnp.transpose(post_anom, (1, 0, 2))[None, None])


def solution(mesh):
    in_specs = (
        P("gx", "gy", None, None, None),
        P("gx", "gy", None, None),
        P("gx", "gy", None, None, None),
        P("gx", "gy", None),
        P("gx", "gy", None),
        P("gx", "gy", None),
        P("gx", "gy", None),
        P("gx", "gy", None),
        P("gx", "gy", None),
    )
    out_specs = (P("gx", "gy", None, None), P("gx", "gy", None, None, None))
    return jax.shard_map(local, mesh=mesh, in_specs=in_specs, out_specs=out_specs, check_vma=False)
```

profile of v0, /device:TPU:4, one launch (start us, length us, event | category | flops | bytes accessed | tf_op | source)
XLA Modules:
  0.0 25.4 jit_solution(10450968239643205221)
XLA Ops:
  0.6 19.0 %exchange.1 = (f32[9,80,128]{2,1,0:T(8,128)}, f32[128,128]{1,0:T(8,128)}, f32[12,80,128]{2,1,0:T(8,128)}, f32[12,128]{1,0:T(8,128)}) custom-call(s32[1,4]{1,0:T(1,128)} %bitcast.20, s32[1,64]{1,0:T(1,128)} %bitcast.21, s32[1,64]{1,0:T(1,128)} %bitcast.22, s32[1,64]{1,0:T(1,128)} %bitcast.23, f32[1,64]{1,0:T(1,128)} %bitcast.24, f32[1,64]{1,0:T(1,128)} %bitcast.25, ...), custom_call_target="tpu_custom_call" | custom-call | tf_op jit(solution)/shard_map/exchange/pallas_call | solution.py:440
  19.6 5.8 %analysis.1 = (f32[13,1,128]{2,1,0:T(1,128)}, f32[13,80,128]{2,1,0:T(8,128)}) custom-call(f32[9,80,128]{2,1,0:T(8,128)} %get-tuple-element.8.tiles_in, f32[128,128]{1,0:T(8,128)} %get-tuple-element.9.metat_in, f32[12,80,128]{2,1,0:T(8,128)} %get-tuple-element.10.fields_in, f32[12,128]{1,0:T(8,128)} %get-tuple-element.11.fmean_in, ...), custom_call_target="tpu_custom_call" | custom-call | tf_op jit(solution)/shard_map/analysis/pallas_call | solution.py:473
where the time goes:
time: 25.5 us; the launch traced here: 25.4 us
  Pallas kernels  24.7 us (97%)
  between operations  0.64 us (3%)
    pallas_call x1, Pallas kernels, local(): pl.pallas_call(exchange_kernel, out_shape=results, in_specs=[anywhere] *...  19 us
    pallas_call x1, Pallas kernels, local(): pl.pallas_call(analysis_kernel, out_shape=(jax.ShapeDtypeStruct((fields +...  5.77 us

commit v1 on v0

--- a/solution.py
+++ b/solution.py
@@ -14,7 +14,7 @@
 NB = 2
 RAD = 2
 CODE = 64
-LIMIT = 65400 * 1024
+LIMIT = 32 * 1024 * 1024
 
 MESH = pl.DeviceIdType.MESH
 OFFS = [(dx, dy) for dx in (-1, 0, 1) for dy in (-1, 0, 1)]
@@ -61,10 +61,10 @@
 
 def exchange_kernel(
     src_ref, order_ref, cell_ref, live_ref, value_ref, error_ref, ocean_ref, weights_ref, atm_ref,
-    tiles_ref, metat_ref, fields_ref, fmean_ref,
+    code_in, move_in, pick_in,
+    tiles_ref, metat_ref, held, fmean, code_ref, move_ref, pick_ref,
     ocn, wts, meta, src, order_in, cell_in, live_in, value_in, error_in,
-    own, blank, metat, held, fmean,
-    local_sem, send_sem, recv_sem, out_sem,
+    local_sem, send_sem, recv_sem,
 ):
     gx, gy = lax.axis_index("gx"), lax.axis_index("gy")
     nx, ny = lax.axis_size("gx"), lax.axis_size("gy")
@@ -84,13 +84,12 @@
     pairs = (
         (ocean_ref, ocn.at[4]), (order_ref, order_in), (cell_ref, cell_in), (live_ref, live_in),
         (value_ref, value_in), (error_ref, error_in), (src_ref, src), (weights_ref, wts),
-        (atm_ref, held),
+        (atm_ref, held), (code_in, code_ref), (move_in, move_ref), (pick_in, pick_ref),
     )
     staged = [pltpu.make_async_copy(x, y, local_sem.at[n]) for n, (x, y) in enumerate(pairs)]
     for copy in staged:
         copy.start()
 
-    blank[...] = jnp.zeros(blank.shape, jnp.float32)
     barrier = pltpu.get_barrier_semaphore()
     for i in OTHERS:
         dx, dy = OFFS[i]
@@ -103,7 +102,7 @@
 
         @pl.when(jnp.logical_not(there(i)))
         def _():
-            pltpu.make_async_copy(blank, tiles_ref.at[i], out_sem.at[i]).start()
+            tiles_ref[i] = jnp.zeros(tiles_ref.shape[1:], jnp.float32)
             meta[i] = jnp.zeros(meta.shape[1:], jnp.float32)
 
     for n in range(9, meta.shape[0]):
@@ -195,7 +194,7 @@
     def column(i):
         dx, dy = OFFS[i]
         return pltpu.make_async_remote_copy(
-            src_ref=own,
+            src_ref=tiles_ref.at[4],
             dst_ref=tiles_ref.at[8 - i],
             send_sem=send_sem.at[2, i],
             recv_sem=recv_sem.at[2, 8 - i],
@@ -232,14 +231,6 @@
         mean = jnp.sum(block, axis=0, keepdims=True) / members
         fmean[v : v + 1, :] = mean
         held[v] = block - mean
-    results = [
-        pltpu.make_async_copy(held, fields_ref, local_sem.at[9]),
-        pltpu.make_async_copy(fmean, fmean_ref, local_sem.at[10]),
-        pltpu.make_async_copy(metat, metat_ref, local_sem.at[11]),
-        pltpu.make_async_copy(own, tiles_ref.at[4], out_sem.at[4]),
-    ]
-    results[0].start()
-    results[1].start()
 
     for at, part in enumerate(parts):
 
@@ -259,8 +250,7 @@
 
     receive(meta, 1)
     flat = meta[...].reshape(meta.shape[0] * meta.shape[1], meta.shape[2])
-    metat[...] = flat.T
-    results[2].start()
+    metat_ref[...] = flat.T
     staged[6].wait()
     staged[7].wait()
 
@@ -283,14 +273,13 @@
         position = (source // ny - gx + 1) * 3 + (source % ny - gy + 1)
         position = jnp.clip(position, 0, 8)
         total += jnp.dot(ocn[position], wts[k], preferred_element_type=jnp.float32)
-    own[...] = total
+    tiles_ref[4] = total
     for i in OTHERS:
 
         @pl.when(there(i))
         def _():
             column(i).start()
 
-    results[3].start()
     for cond, copy in firsts + relays + [hand[2:] for hand in hands]:
 
         @pl.when(cond)
@@ -298,14 +287,10 @@
             copy.wait_send()
 
     settle(meta, 1)
-    for copy in results:
+    for copy in staged[9:]:
         copy.wait()
     for i in OTHERS:
 
-        @pl.when(jnp.logical_not(there(i)))
-        def _():
-            pltpu.make_async_copy(blank, tiles_ref.at[i], out_sem.at[i]).wait()
-
         @pl.when(there(i))
         def _():
             column(i).wait_send()
@@ -313,21 +298,11 @@
 
 
 def analysis_kernel(
-    tiles_in, metat_in, fields_in, fmean_in, code_in, move_in, pick_in,
+    tiles_ref, metat_ref, fields_in, fmean_ref, code_ref, move_ref, pick_ref,
     mean_ref, anom_ref,
-    tiles_ref, metat_ref, fmean_ref, code_ref, move_ref, pick_ref, held, shifted, local_sem, out_sem,
+    held, shifted, out_sem,
 ):
     fields, members, cells = fields_in.shape
-    pairs = (
-        (tiles_in, tiles_ref), (metat_in, metat_ref), (fmean_in, fmean_ref),
-        (fields_in, held.at[0:fields]), (pick_in, pick_ref), (code_in, code_ref),
-        (move_in, move_ref),
-    )
-    staged = [pltpu.make_async_copy(x, y, local_sem.at[n]) for n, (x, y) in enumerate(pairs)]
-    for n in (0, 4, 1, 5, 6, 2, 3):
-        staged[n].start()
-    staged[0].wait()
-    staged[4].wait()
 
     scale = 1.0 / (members - 1)
     beside = split_rows(jnp.concatenate([tiles_ref[i] for i in OTHERS], axis=1))
@@ -335,8 +310,6 @@
     grid = jnp.concatenate([tiles_ref[4], halo[:members] + halo[members:]], axis=1)
     gmean = jnp.sum(grid, axis=0, keepdims=True) / members
     grid = grid - gmean
-    staged[1].wait()
-    staged[5].wait()
     code = code_ref[0:1, :]
 
     for b in range(NB):
@@ -362,8 +335,6 @@
         alpha = jnp.sum(gains, axis=0, keepdims=True)
         beta = jnp.sum(sums, axis=0, keepdims=True) - gmean * jnp.sum(weights, axis=0, keepdims=True)
         extra = jnp.concatenate([alpha, beta, jnp.zeros((6, 2 * cells), jnp.float32)], axis=0)
-        if b == 0:
-            staged[6].wait()
         left = split_rows(jnp.concatenate([grid, extra], axis=0))
         width = (8 if last else 16) * cells
         moved = jnp.dot(left, move_ref[:, :width], preferred_element_type=jnp.float32)
@@ -390,13 +361,10 @@
 
         own = grid[:, :cells]
         held[fields] = own
-        if b == 0:
-            staged[2].wait()
-            staged[3].wait()
         own_args = (alpha[:, :cells], beta[:, :cells])
 
         def one_field(v, carry, own_args=own_args, last=last, b=b, step=step):
-            block, mean = step(held[v], 0, held[fields], *own_args)
+            block, mean = step(fields_in[v] if b == 0 else held[v], 0, held[fields], *own_args)
             held[v] = block
             before = fmean_ref[pl.ds(v, 1), :] if b == 0 else mean_ref[v]
             mean_ref[v] = before + mean
@@ -432,16 +400,19 @@
     anywhere = pl.BlockSpec(memory_space=pl.ANY)
     code, move, pick = tables()
     results = (
-        jax.ShapeDtypeStruct((9, members, cells), jnp.float32),
-        jax.ShapeDtypeStruct((128, 128), jnp.float32),
-        jax.ShapeDtypeStruct((fields, members, cells), jnp.float32),
-        jax.ShapeDtypeStruct((fields, cells), jnp.float32),
+        pltpu.VMEM((9, members, cells), jnp.float32),
+        pltpu.VMEM((128, 128), jnp.float32),
+        pltpu.VMEM((fields, members, cells), jnp.float32),
+        pltpu.VMEM((fields, cells), jnp.float32),
+        pltpu.VMEM(code.shape, jnp.float32),
+        pltpu.VMEM(move.shape, jnp.bfloat16),
+        pltpu.VMEM(pick.shape, jnp.bfloat16),
     )
     state = pl.pallas_call(
         exchange_kernel,
         out_shape=results,
-        in_specs=[anywhere] * 9,
-        out_specs=(anywhere,) * 4,
+        in_specs=[anywhere] * 12,
+        out_specs=(vmem,) * 7,
         scratch_shapes=[
             pltpu.VMEM((9, members, depth), jnp.bfloat16),
             pltpu.VMEM((sources, depth, cells), jnp.bfloat16),
@@ -452,23 +423,24 @@
             pltpu.VMEM((1, slots), jnp.int32),
             pltpu.VMEM((1, slots), jnp.float32),
             pltpu.VMEM((1, slots), jnp.float32),
-            pltpu.VMEM((members, cells), jnp.float32),
-            pltpu.VMEM((members, cells), jnp.float32),
-            pltpu.VMEM((128, 128), jnp.float32),
-            pltpu.VMEM((fields, members, cells), jnp.float32),
-            pltpu.VMEM((fields, cells), jnp.float32),
             pltpu.SemaphoreType.DMA((12,)),
             pltpu.SemaphoreType.DMA((4, 9)),
             pltpu.SemaphoreType.DMA((4, 9)),
-            pltpu.SemaphoreType.DMA((9,)),
         ],
         compiler_params=pltpu.CompilerParams(
             collective_id=0, has_side_effects=True, vmem_limit_bytes=LIMIT
         ),
         name="exchange",
     )(
-        pair_src[0], obs_order[0], obs_cell[0], obs_live[0], obs_value[0], obs_error[0],
-        ocean_members[0, 0], remap_weights[0, 0], jnp.transpose(atm_members[0, 0], (1, 0, 2)),
+        *(
+            pltpu.with_memory_space_constraint(x, pltpu.HBM)
+            for x in (
+                pair_src[0], obs_order[0], obs_cell[0], obs_live[0], obs_value[0], obs_error[0],
+                ocean_members[0, 0], remap_weights[0, 0],
+                jnp.transpose(atm_members[0, 0], (1, 0, 2)),
+                jnp.asarray(code), jnp.asarray(move, jnp.bfloat16), jnp.asarray(pick, jnp.bfloat16),
+            )
+        )
     )
     post_mean, post_anom = pl.pallas_call(
         analysis_kernel,
@@ -476,21 +448,16 @@
             jax.ShapeDtypeStruct((fields + 1, 1, cells), jnp.float32),
             jax.ShapeDtypeStruct((fields + 1, members, cells), jnp.float32),
         ),
-        in_specs=[anywhere] * 7,
+        in_specs=[vmem] * 7,
         out_specs=(vmem, anywhere),
         scratch_shapes=[
-            *(pltpu.VMEM(r.shape, jnp.float32) for r in (results[0], results[1], results[3])),
-            pltpu.VMEM(code.shape, jnp.float32),
-            pltpu.VMEM(move.shape, jnp.bfloat16),
-            pltpu.VMEM(pick.shape, jnp.bfloat16),
             pltpu.VMEM((fields + 1, members, cells), jnp.float32),
             pltpu.VMEM((members + 8, 16 * cells), jnp.float32),
-            pltpu.SemaphoreType.DMA((7,)),
             pltpu.SemaphoreType.DMA((fields + 1,)),
         ],
         compiler_params=pltpu.CompilerParams(vmem_limit_bytes=LIMIT),
         name="analysis",
-    )(*state, jnp.asarray(code), jnp.asarray(move, jnp.bfloat16), jnp.asarray(pick, jnp.bfloat16))
+    )(*state)
     return (post_mean.reshape(1, 1, fields + 1, cells), jnp.transpose(post_anom, (1, 0, 2))[None, None])
 
 

time: 25.5 us -> 24.1 us (0.945)
  Pallas kernels: 24.7 us -> 23.3 us
    pallas_call x1, Pallas kernels: 5.77 us -> 4.48 us  [local(): pl.pallas_call(analysis_kernel, out_shape=(jax.ShapeDtypeStruct((fields +...]
where the time goes in v1:
time: 24.1 us; the launch traced here: 23.9 us
  Pallas kernels  23.3 us (97%)
  between operations  0.64 us (3%)
    pallas_call x1, Pallas kernels, local(): pl.pallas_call(exchange_kernel, out_shape=results, in_specs=[anywhere] *...  18.8 us
    pallas_call x1, Pallas kernels, local(): pl.pallas_call(analysis_kernel, out_shape=(jax.ShapeDtypeStruct((fields +...  4.48 us

profile of v1, /device:TPU:4, one launch (start us, length us, event | category | flops | bytes accessed | tf_op | source)
XLA Modules:
  0.0 23.9 jit_solution(9384361138640386983)
XLA Ops:
  0.6 18.8 %exchange.1 = (f32[9,80,128]{2,1,0:T(8,128)S(1)}, f32[128,128]{1,0:T(8,128)S(1)}, f32[12,80,128]{2,1,0:T(8,128)S(1)}, f32[12,128]{1,0:T(8,128)S(1)}, f32[8,256]{...) custom-call(s32[1,4]{1,0:T(1,128)} %bitcast.20, s32[1,64]{1,0:T(1,128)} %bitcast.21, ...), custom_call_target="tpu_custom_call" | custom-call | tf_op jit(solution)/shard_map/exchange/pallas_call | solution.py:411
  19.4 4.5 %analysis.1 = (f32[13,1,128]{2,1,0:T(1,128)}, f32[13,80,128]{2,1,0:T(8,128)}) custom-call(f32[9,80,128]{2,1,0:T(8,128)S(1)} %get-tuple-element.11.tiles_ref, f32[128,128]{1,0:T(8,128)S(1)} %get-tuple-element.12.metat_ref, f32[12,80,128]{2,1,0:T(8,128)S(1)} %get-tuple-element.13.fields_in, f32[12,128]{1,0:T(8,128)S(1)} %get-tuple-element.14.fmean_ref, ...), custom_call_target="tpu_custom_call" | custom-call | tf_op jit(solution)/shard_map/analysis/pallas_call | solution.py:445

commit v2 on v1

--- a/solution.py
+++ b/solution.py
@@ -19,39 +19,58 @@
 MESH = pl.DeviceIdType.MESH
 OFFS = [(dx, dy) for dx in (-1, 0, 1) for dy in (-1, 0, 1)]
 OTHERS = [i for i in range(9) if i != 4]
+NEAR = [1, 3, 5, 7]
+FAR = [0, 2, 6, 8]
+PIECE = 16
+SHARE = 4
 
 
 def taper_of(dx, dy):
     return max(1.0 - (dx * dx + dy * dy) / float(RAD * RAD), 0.0) ** 2
+
+
+def edge(d, size):
+    return {-1: range(RAD), 0: range(size), 1: range(size - RAD, size)}[d]
+
+
+def strip(i):
+    dx, dy = OFFS[i]
+    return [(x, y) for x in edge(dx, AX) for y in edge(dy, AY)]
+
+
+def strips():
+    spans, at = {}, 0
+    for i in OTHERS:
+        rows = -(-len(strip(i)) // 8) * 8
+        spans[i] = (at, rows)
+        at += rows
+    return spans
+
+
+SPANS = strips()
 
 
 @functools.lru_cache
 def tables():
     cells = AX * AY
-    own = [(c // AY, c % AY) for c in range(cells)]
-    halo = [
-        (x, y)
-        for x in range(-RAD, AX + RAD)
-        for y in range(-RAD, AY + RAD)
-        if not (0 <= x < AX and 0 <= y < AY)
-    ]
-    lanes = own + halo
-    where = {xy: n for n, xy in enumerate(lanes)}
+    where = {(c // AY, c % AY): c for c in range(cells)}
+    out = np.zeros((cells, cells), np.float32)
+    for i in OTHERS:
+        dx, dy = OFFS[i]
+        for n, (x, y) in enumerate(strip(i)):
+            out[SPANS[i][0] + n, x * AY + y] = 1.0
+        for n, (x, y) in enumerate(strip(8 - i)):
+            where[(x + dx * AX, y + dy * AY)] = cells + SPANS[i][0] + n
     code = np.full((8, 2 * cells), -1.0, np.float32)
-    for n, (x, y) in enumerate(lanes):
+    move = np.zeros((2 * cells, 2, 8, cells), np.float32)
+    for (x, y), n in where.items():
         code[:, n] = (x + AX) * CODE + (y + AY)
-    move = np.zeros((2 * cells, 2, 8, cells), np.float32)
-    for n, (x, y) in enumerate(lanes):
         for d, i in enumerate(OTHERS):
             dx, dy = OFFS[i]
             src = where.get((x + dx, y + dy))
             if src is not None:
                 move[src, n // cells, d, n % cells] = 1.0
-    pick = np.zeros((8, cells, cells), np.float32)
-    for n, (x, y) in enumerate(halo):
-        i = (x // AX + 1) * 3 + (y // AY + 1)
-        pick[OTHERS.index(i), (x % AX) * AY + (y % AY), n] = 1.0
-    return code, move.reshape(2 * cells, 16 * cells), pick.reshape(8 * cells, cells)
+    return code, move.reshape(2 * cells, 16 * cells), out
 
 
 def split_rows(block):
@@ -61,14 +80,14 @@
 
 def exchange_kernel(
     src_ref, order_ref, cell_ref, live_ref, value_ref, error_ref, ocean_ref, weights_ref, atm_ref,
-    code_in, move_in, pick_in,
-    tiles_ref, metat_ref, held, fmean, code_ref, move_ref, pick_ref,
-    ocn, wts, meta, src, order_in, cell_in, live_in, value_in, error_in,
-    local_sem, send_sem, recv_sem,
+    code_in, move_in, out_in,
+    own_ref, halo_ref, metat_ref, held, fmean, code_ref, move_ref,
+    ocn, wts, meta, src, order_in, cell_in, live_in, value_in, error_in, out, strip_ref,
+    local_sem, send_sem, recv_sem, note_sem,
 ):
     gx, gy = lax.axis_index("gx"), lax.axis_index("gy")
     nx, ny = lax.axis_size("gx"), lax.axis_size("gy")
-    members = tiles_ref.shape[1]
+    members = own_ref.shape[0]
     fields = atm_ref.shape[0]
     slots = order_in.shape[1]
 
@@ -84,14 +103,14 @@
     pairs = (
         (ocean_ref, ocn.at[4]), (order_ref, order_in), (cell_ref, cell_in), (live_ref, live_in),
         (value_ref, value_in), (error_ref, error_in), (src_ref, src), (weights_ref, wts),
-        (atm_ref, held), (code_in, code_ref), (move_in, move_ref), (pick_in, pick_ref),
+        (atm_ref, held), (code_in, code_ref), (move_in, move_ref), (out_in, out),
     )
     staged = [pltpu.make_async_copy(x, y, local_sem.at[n]) for n, (x, y) in enumerate(pairs)]
     for copy in staged:
         copy.start()
 
     barrier = pltpu.get_barrier_semaphore()
-    for i in OTHERS:
+    for i in NEAR:
         dx, dy = OFFS[i]
 
         @pl.when(there(i))
@@ -102,7 +121,8 @@
 
         @pl.when(jnp.logical_not(there(i)))
         def _():
-            tiles_ref[i] = jnp.zeros(tiles_ref.shape[1:], jnp.float32)
+            at, rows = SPANS[i]
+            halo_ref[at : at + rows, :] = jnp.zeros((rows, halo_ref.shape[1]), jnp.float32)
             meta[i] = jnp.zeros(meta.shape[1:], jnp.float32)
 
     for n in range(9, meta.shape[0]):
@@ -125,105 +145,101 @@
     meta[4] = jnp.concatenate([rows, jnp.zeros((8, meta.shape[2] - slots), jnp.float32)], axis=1)
 
     staged[0].wait()
-    across = 1 + has_x(-1).astype(jnp.int32) + has_x(1).astype(jnp.int32)
-    along = 1 + has_y(-1).astype(jnp.int32) + has_y(1).astype(jnp.int32)
-    pl.semaphore_wait(barrier, across * along - 1)
+    pl.semaphore_wait(barrier, sum(there(i).astype(jnp.int32) for i in NEAR))
 
     outer = lax.rem(gy, 2) * 2 - 1
-
-    first = (members // 2 + 15) // 16 * 16
-    parts = ((0, 0, first), (3, first, members - first))
-
-    def ocean(part, source, target, n, dx, dy):
-        kind, low, size = part
+    count = members // PIECE
+
+    def relayed(y, p):
+        at = lax.rem(y + 8, 8)
+        return ((at == 2) | (at == 5)) if p >= SHARE else ((at != 1) & (at != 6))
+
+    def ocean(p, source, target, kind, dx, dy, shared=False):
         return pltpu.make_async_remote_copy(
-            src_ref=ocn.at[source, pl.ds(low, size)],
-            dst_ref=ocn.at[target, pl.ds(low, size)],
-            send_sem=send_sem.at[kind, n],
-            recv_sem=recv_sem.at[kind, target],
+            src_ref=ocn.at[source, pl.ds(p * PIECE, PIECE)],
+            dst_ref=ocn.at[target, pl.ds(p * PIECE, PIECE)],
+            send_sem=send_sem.at[kind, p],
+            recv_sem=recv_sem.at[target, 0 if shared else p],
             device_id=(gx + dx, gy + dy),
             device_id_type=MESH,
         )
 
-    def arrive(part, at, dx, dy):
-        ocean(part, at, at, 4, dx, dy).wait_recv()
-
-    firsts = [
-        (cond, ocean(part, 4, target, n, dx, dy))
-        for part in parts
-        for cond, target, n, dx, dy in (
-            (has_y(outer), 4 - outer, 1, 0, outer),
-            (has_x(-1), 7, 2, -1, 0),
-            (has_x(1), 1, 3, 1, 0),
-            (has_y(-outer), 4 + outer, 0, 0, -outer),
-        )
+    def arrive(p, at, dx, dy):
+        ocean(p, at, at, 0, dx, dy).wait_recv()
+
+    def arrive_all(at, dx, dy):
+        pltpu.make_async_remote_copy(
+            src_ref=ocn.at[at],
+            dst_ref=ocn.at[at],
+            send_sem=send_sem.at[0, 0],
+            recv_sem=recv_sem.at[at, 0],
+            device_id=(gx + dx, gy + dy),
+            device_id_type=MESH,
+        ).wait_recv()
+
+    order = range(count)
+    sends = [
+        (has_y(outer), [ocean(p, 4, 4 - outer, 1, 0, outer) for p in order]),
+        (has_x(-1), [ocean(p, 4, 7, 2, -1, 0) for p in reversed(order)]),
+        (has_x(1), [ocean(p, 4, 1, 3, 1, 0) for p in reversed(order)]),
+        (has_y(-outer), [ocean(p, 4, 4 + outer, 0, 0, -outer, True) for p in order]),
     ]
-    relays = [
-        (has_y(outer) & has_x(dx), ocean(part, 4 + outer, 4 - 3 * dx + outer, n, dx, 0))
-        for part in parts
-        for dx, n in ((-1, 5), (1, 6))
-    ]
-    hands = [
-        (
-            part, dx, has_x(dx) & has_y(-outer),
-            ocean(part, 4 + 3 * dx, 4 + 3 * dx + outer, n, 0, -outer),
-        )
-        for part in parts
-        for dx, n in ((-1, 7), (1, 8))
-    ]
-
-    def begin(cond, copy):
+    for cond, copies in sends:
+
         @pl.when(cond)
         def _():
-            copy.start()
-
-    for cond, copy in firsts:
-        begin(cond, copy)
-
-    def remote(buf, kind, i):
+            for copy in copies:
+                copy.start()
+
+    def relay(p, dx):
+        return ocean(p, 4 + outer, 4 - 3 * dx + outer, 4 if dx < 0 else 5, dx, 0, True)
+
+    def forward(p, dx):
+        return ocean(p, 4 + 3 * dx, 4 + 3 * dx - outer, 6 if dx < 0 else 7, 0, outer, True)
+
+    def hand(p, dx):
+        return ocean(p, 4 + 3 * dx, 4 + 3 * dx + outer, 8 if dx < 0 else 9, 0, -outer, True)
+
+    for p in order:
+        for dx in (-1, 1):
+            sends.append((has_x(dx) & has_y(outer) & relayed(gy + outer, p), [relay(p, dx)]))
+            sends.append(
+                (has_x(dx) & has_y(outer) & jnp.logical_not(relayed(gy, p)), [forward(p, dx)])
+            )
+    for dx in (-1, 1):
+        sends.append((has_x(dx) & has_y(-outer), [hand(p, dx) for p in order]))
+
+    def remote(i):
         dx, dy = OFFS[i]
         return pltpu.make_async_remote_copy(
-            src_ref=buf.at[4],
-            dst_ref=buf.at[8 - i],
-            send_sem=send_sem.at[kind, i],
-            recv_sem=recv_sem.at[kind, 8 - i],
+            src_ref=meta.at[4],
+            dst_ref=meta.at[8 - i],
+            send_sem=note_sem.at[0, i],
+            recv_sem=note_sem.at[1, 8 - i],
             device_id=(gx + dx, gy + dy),
             device_id_type=MESH,
         )
 
-    def column(i):
+    def border(i):
         dx, dy = OFFS[i]
+        (source, rows), (target, _) = SPANS[i], SPANS[8 - i]
         return pltpu.make_async_remote_copy(
-            src_ref=tiles_ref.at[4],
-            dst_ref=tiles_ref.at[8 - i],
-            send_sem=send_sem.at[2, i],
-            recv_sem=recv_sem.at[2, 8 - i],
+            src_ref=strip_ref.at[pl.ds(source, rows)],
+            dst_ref=halo_ref.at[pl.ds(target, rows)],
+            send_sem=note_sem.at[2, i],
+            recv_sem=note_sem.at[3, 8 - i],
             device_id=(gx + dx, gy + dy),
             device_id_type=MESH,
         )
 
-    def send(buf, kind):
-        for i in OTHERS:
+    def each(which, act):
+        for i in which:
 
             @pl.when(there(i))
             def _():
-                remote(buf, kind, i).start()
-
-    def receive(buf, kind):
-        for i in OTHERS:
-
-            @pl.when(there(i))
-            def _():
-                remote(buf, kind, 8 - i).wait_recv()
-
-    def settle(buf, kind):
-        for i in OTHERS:
-
-            @pl.when(there(i))
-            def _():
-                remote(buf, kind, i).wait_send()
-
-    send(meta, 1)
+                act(i)
+
+    each(NEAR, lambda i: remote(i).start())
 
     staged[8].wait()
     for v in range(fields):
@@ -232,82 +248,92 @@
         fmean[v : v + 1, :] = mean
         held[v] = block - mean
 
-    for at, part in enumerate(parts):
+    for p in order:
+        back = count - 1 - p
+        for dx in (-1, 1):
+
+            @pl.when(has_x(dx))
+            def _():
+                arrive(back, 4 + 3 * dx, dx, 0)
+
+                @pl.when(has_y(outer) & jnp.logical_not(relayed(gy, back)))
+                def _():
+                    forward(back, dx).start()
+
+                @pl.when(has_y(-outer))
+                def _():
+                    hand(back, dx).start()
+
+        if p == 0:
+            each(FAR, lambda i: remote(i).start())
 
         @pl.when(has_y(outer))
         def _():
-            arrive(part, 4 + outer, 0, outer)
-
-        for cond, copy in relays[2 * at : 2 * at + 2]:
-            begin(cond, copy)
-    for part, dx, cond, copy in hands:
-
-        @pl.when(has_x(dx))
-        def _():
-            arrive(part, 4 + 3 * dx, dx, 0)
-
-        begin(cond, copy)
-
-    receive(meta, 1)
+            arrive(p, 4 + outer, 0, outer)
+
+            @pl.when(relayed(gy + outer, p))
+            def _():
+                for dx in (-1, 1):
+
+                    @pl.when(has_x(dx))
+                    def _():
+                        relay(p, dx).start()
+
+    each(OTHERS, lambda i: remote(8 - i).wait_recv())
     flat = meta[...].reshape(meta.shape[0] * meta.shape[1], meta.shape[2])
     metat_ref[...] = flat.T
     staged[6].wait()
     staged[7].wait()
-
-    for part in parts:
-
-        @pl.when(has_y(-outer))
-        def _():
-            arrive(part, 4 - outer, 0, -outer)
-
-        for dx in (-1, 1):
-            for dy in (outer, -outer):
-
-                @pl.when(has_x(dx) & has_y(dy))
-                def _():
-                    arrive(part, 4 + 3 * dx + dy, dx, 0)
-
-    total = jnp.zeros(tiles_ref.shape[1:], jnp.float32)
+    staged[11].wait()
+
+    @pl.when(has_y(-outer))
+    def _():
+        arrive_all(4 - outer, 0, -outer)
+
+    for dx in (-1, 1):
+        for dy in (-outer, outer):
+
+            @pl.when(has_x(dx) & has_y(dy))
+            def _():
+                arrive_all(4 + 3 * dx + dy, dx, 0)
+
+    total = jnp.zeros(own_ref.shape, jnp.float32)
     for k in range(wts.shape[0]):
         source = src[0, k]
         position = (source // ny - gx + 1) * 3 + (source % ny - gy + 1)
         position = jnp.clip(position, 0, 8)
         total += jnp.dot(ocn[position], wts[k], preferred_element_type=jnp.float32)
-    tiles_ref[4] = total
-    for i in OTHERS:
-
-        @pl.when(there(i))
-        def _():
-            column(i).start()
-
-    for cond, copy in firsts + relays + [hand[2:] for hand in hands]:
+    own_ref[...] = total
+    rest = jnp.zeros((out.shape[0] - members, total.shape[1]), jnp.float32)
+    picked = lax.dot_general(
+        out[...], split_rows(jnp.concatenate([total, rest], axis=0)), (((1,), (1,)), ((), ())),
+        preferred_element_type=jnp.float32,
+    )
+    strip_ref[...] = picked[:, : out.shape[0]] + picked[:, out.shape[0] :]
+    each(FAR + NEAR, lambda i: border(i).start())
+    for cond, copies in sends:
 
         @pl.when(cond)
         def _():
-            copy.wait_send()
-
-    settle(meta, 1)
-    for copy in staged[9:]:
+            for copy in copies:
+                copy.wait_send()
+
+    each(OTHERS, lambda i: remote(i).wait_send())
+    for copy in staged[9:11]:
         copy.wait()
-    for i in OTHERS:
-
-        @pl.when(there(i))
-        def _():
-            column(i).wait_send()
-            column(8 - i).wait_recv()
+    each(OTHERS, lambda i: border(i).wait_send())
+    each(OTHERS, lambda i: border(8 - i).wait_recv())
 
 
 def analysis_kernel(
-    tiles_ref, metat_ref, fields_in, fmean_ref, code_ref, move_ref, pick_ref,
+    own_ref, halo_ref, metat_ref, fields_in, fmean_ref, code_ref, move_ref,
     mean_ref, anom_ref,
     held, shifted, out_sem,
 ):
     fields, members, cells = fields_in.shape
 
     scale = 1.0 / (members - 1)
-    beside = split_rows(jnp.concatenate([tiles_ref[i] for i in OTHERS], axis=1))
-    halo = jnp.dot(beside, pick_ref[...], preferred_element_type=jnp.float32)
-    grid = jnp.concatenate([tiles_ref[4], halo[:members] + halo[members:]], axis=1)
+    grid = jnp.concatenate([own_ref[...], halo_ref[...].T[:members]], axis=1)
     gmean = jnp.sum(grid, axis=0, keepdims=True) / members
     grid = grid - gmean
     code = code_ref[0:1, :]
@@ -398,15 +424,15 @@
     sources, depth = remap_weights.shape[2:4]
     vmem = pl.BlockSpec(memory_space=pltpu.VMEM)
     anywhere = pl.BlockSpec(memory_space=pl.ANY)
-    code, move, pick = tables()
+    code, move, out = tables()
     results = (
-        pltpu.VMEM((9, members, cells), jnp.float32),
+        pltpu.VMEM((members, cells), jnp.float32),
+        pltpu.VMEM((cells, 128), jnp.float32),
         pltpu.VMEM((128, 128), jnp.float32),
         pltpu.VMEM((fields, members, cells), jnp.float32),
         pltpu.VMEM((fields, cells), jnp.float32),
         pltpu.VMEM(code.shape, jnp.float32),
         pltpu.VMEM(move.shape, jnp.bfloat16),
-        pltpu.VMEM(pick.shape, jnp.bfloat16),
     )
     state = pl.pallas_call(
         exchange_kernel,
@@ -423,8 +449,11 @@
             pltpu.VMEM((1, slots), jnp.int32),
             pltpu.VMEM((1, slots), jnp.float32),
             pltpu.VMEM((1, slots), jnp.float32),
+            pltpu.VMEM(out.shape, jnp.bfloat16),
+            pltpu.VMEM((cells, 128), jnp.float32),
             pltpu.SemaphoreType.DMA((12,)),
-            pltpu.SemaphoreType.DMA((4, 9)),
+            pltpu.SemaphoreType.DMA((10, members // PIECE)),
+            pltpu.SemaphoreType.DMA((9, members // PIECE)),
             pltpu.SemaphoreType.DMA((4, 9)),
         ],
         compiler_params=pltpu.CompilerParams(
@@ -438,7 +467,7 @@
                 pair_src[0], obs_order[0], obs_cell[0], obs_live[0], obs_value[0], obs_error[0],
                 ocean_members[0, 0], remap_weights[0, 0],
                 jnp.transpose(atm_members[0, 0], (1, 0, 2)),
-                jnp.asarray(code), jnp.asarray(move, jnp.bfloat16), jnp.asarray(pick, jnp.bfloat16),
+                jnp.asarray(code), jnp.asarray(move, jnp.bfloat16), jnp.asarray(out, jnp.bfloat16),
             )
         )
     )

time: 24.1 us -> 21.6 us (0.90)
  the two profiles are of different devices: /device:TPU:4 before, /device:TPU:3 now
where the time goes in v2:
time: 21.6 us; the launch traced here: 21.4 us
  Pallas kernels  20.7 us (96%)
  between operations  0.64 us (3%)
    pallas_call x1, Pallas kernels, local(): pl.pallas_call(exchange_kernel, out_shape=results, in_specs=[anywhere] *...  16.2 us
    pallas_call x1, Pallas kernels, local(): pl.pallas_call(analysis_kernel, out_shape=(jax.ShapeDtypeStruct((fields +...  4.49 us

profile of v2, /device:TPU:3, one launch (start us, length us, event | category | flops | bytes accessed | tf_op | source)
XLA Modules:
  0.0 21.4 jit_solution(16328695326534795857)
XLA Ops:
  0.6 16.2 %exchange.1 = (f32[80,128]{1,0:T(8,128)S(1)}, f32[128,128]{1,0:T(8,128)S(1)}, f32[128,128]{1,0:T(8,128)S(1)}, f32[12,80,128]{2,1,0:T(8,128)S(1)}, f32[12,128]{1,...) custom-call(s32[1,4]{1,0:T(1,128)} %bitcast.20, s32[1,64]{1,0:T(1,128)} %bitcast.21, ...), custom_call_target="tpu_custom_call" | custom-call | tf_op jit(solution)/shard_map/exchange/pallas_call | solution.py:437
  16.9 4.5 %analysis.1 = (f32[13,1,128]{2,1,0:T(1,128)}, f32[13,80,128]{2,1,0:T(8,128)}) custom-call(f32[80,128]{1,0:T(8,128)S(1)} %get-tuple-element.11.own_ref, f32[128,128]{1,0:T(8,128)S(1)} %get-tuple-element.12.halo_ref, f32[128,128]{1,0:T(8,128)S(1)} %get-tuple-element.13.metat_ref, f32[12,80,128]{2,1,0:T(8,128)S(1)} %get-tuple-element.14.fields_in, ...), custom_call_target="tpu_custom_call" | custom-call | tf_op jit(solution)/shard_map/analysis/pallas_call | solution.py:474

commit v3 on v2

--- a/solution.py
+++ b/solution.py
@@ -23,6 +23,7 @@
 FAR = [0, 2, 6, 8]
 PIECE = 16
 SHARE = 4
+SLOTS = 5
 
 
 def taper_of(dx, dy):
@@ -62,15 +63,25 @@
         for n, (x, y) in enumerate(strip(8 - i)):
             where[(x + dx * AX, y + dy * AY)] = cells + SPANS[i][0] + n
     code = np.full((8, 2 * cells), -1.0, np.float32)
+    code[1:, :] = 0.0
     move = np.zeros((2 * cells, 2, 8, cells), np.float32)
+    slot = np.zeros((2 * cells, SLOTS, cells), np.float32)
     for (x, y), n in where.items():
-        code[:, n] = (x + AX) * CODE + (y + AY)
+        code[0, n] = (x + AX) * CODE + (y + AY)
+        taken = 0
         for d, i in enumerate(OTHERS):
             dx, dy = OFFS[i]
             src = where.get((x + dx, y + dy))
             if src is not None:
                 move[src, n // cells, d, n % cells] = 1.0
-    return code, move.reshape(2 * cells, 16 * cells), out
+                if n < cells <= src:
+                    slot[src, taken, n] = 1.0
+                    code[1 + taken, n] = taper_of(dx, dy)
+                    taken += 1
+    own = move[:, 0].reshape(2 * cells, 8 * cells)
+    far = move[:, 1].reshape(2 * cells, 8 * cells)
+    slot = slot.reshape(2 * cells, SLOTS * cells)
+    return code, own, far, slot, out
 
 
 def split_rows(block):
@@ -78,11 +89,64 @@
     return jnp.concatenate([high, block - high], axis=0).astype(jnp.bfloat16)
 
 
+def moments(block, members):
+    mean = jnp.sum(block, axis=0, keepdims=True) / members
+    return mean, block - mean
+
+
+def strengths(block, mean, table, members):
+    variance = jnp.sum(block * block, axis=0, keepdims=True) / (members - 1)
+    live, error, value, base = table
+    denom = variance + base
+    weighting = live / denom
+    damping = 1.0 / (1.0 + jnp.sqrt(error / denom))
+    alpha = jnp.sum(weighting * damping, axis=0, keepdims=True)
+    beta = jnp.sum(weighting * value, axis=0, keepdims=True)
+    return alpha, beta - mean * jnp.sum(weighting, axis=0, keepdims=True)
+
+
+def shift(block, alpha, beta, tables):
+    rest = jnp.zeros((6, block.shape[1]), jnp.float32)
+    rows = block.shape[0] + 8
+    left = split_rows(jnp.concatenate([block, alpha, beta, rest], axis=0))
+    moved = jnp.dot(left, tables, preferred_element_type=jnp.float32)
+    return moved[:rows] + moved[rows:]
+
+
+def gather(block, sources):
+    total = jnp.zeros_like(block)
+    mean = jnp.zeros((1, block.shape[1]), jnp.float32)
+    for source, a, m in sources:
+        cov = jnp.sum(block * source, axis=0, keepdims=True)
+        mean = mean + cov * m
+        total = total + source * (cov * a)
+    return total, mean
+
+
+def sources_of(shifted, members, weights):
+    cells = weights[0][1]
+    found = []
+    for d, (weight, width) in enumerate(weights):
+        part = slice(d * cells, d * cells + width)
+        found.append(
+            (
+                shifted[:members, part],
+                shifted[members : members + 1, part] * weight,
+                shifted[members + 1 : members + 2, part] * weight,
+            )
+        )
+    return found
+
+
+def around(scale, cells):
+    return [(scale * taper_of(*OFFS[i]), cells) for i in OTHERS]
+
+
 def exchange_kernel(
     src_ref, order_ref, cell_ref, live_ref, value_ref, error_ref, ocean_ref, weights_ref, atm_ref,
-    code_in, move_in, out_in,
-    own_ref, halo_ref, metat_ref, held, fmean, code_ref, move_ref,
-    ocn, wts, meta, src, order_in, cell_in, live_in, value_in, error_in, out, strip_ref,
+    code_in, near_in, far_in, slot_in, out_in,
+    own_ref, halo_ref, obs_ref, held, part_ref, fmean, beyond_ref, code_ref, near_ref, far_ref, slot_ref,
+    ocn, wts, meta, src, order_in, cell_in, live_in, value_in, error_in, out, strip_ref, shifted,
     local_sem, send_sem, recv_sem, note_sem,
 ):
     gx, gy = lax.axis_index("gx"), lax.axis_index("gy")
@@ -103,7 +167,8 @@
     pairs = (
         (ocean_ref, ocn.at[4]), (order_ref, order_in), (cell_ref, cell_in), (live_ref, live_in),
         (value_ref, value_in), (error_ref, error_in), (src_ref, src), (weights_ref, wts),
-        (atm_ref, held), (code_in, code_ref), (move_in, move_ref), (out_in, out),
+        (atm_ref, held), (code_in, code_ref), (out_in, out), (near_in, near_ref),
+        (far_in, far_ref), (slot_in, slot_ref),
     )
     staged = [pltpu.make_async_copy(x, y, local_sem.at[n]) for n, (x, y) in enumerate(pairs)]
     for copy in staged:
@@ -280,11 +345,9 @@
                         relay(p, dx).start()
 
     each(OTHERS, lambda i: remote(8 - i).wait_recv())
-    flat = meta[...].reshape(meta.shape[0] * meta.shape[1], meta.shape[2])
-    metat_ref[...] = flat.T
     staged[6].wait()
     staged[7].wait()
-    staged[11].wait()
+    staged[10].wait()
 
     @pl.when(has_y(-outer))
     def _():
@@ -311,6 +374,52 @@
     )
     strip_ref[...] = picked[:, : out.shape[0]] + picked[:, out.shape[0] :]
     each(FAR + NEAR, lambda i: border(i).start())
+
+    flat = meta[...].reshape(meta.shape[0] * meta.shape[1], meta.shape[2]).T
+    cells = total.shape[1]
+    staged[9].wait()
+    for b in range(NB):
+        for half, tiles in ((0, [4]), (1, OTHERS)):
+            code = code_ref[0:1, half * cells : (half + 1) * cells]
+            live = jnp.zeros((OB, cells), jnp.float32)
+            error = live + 1.0
+            value = live
+            base = live + 1.0
+            for i in tiles:
+                dx, dy = OFFS[i]
+                column = flat[b * OB : (b + 1) * OB, 8 * i : 8 * i + 4]
+                hit = column[:, 0:1] + float((AX * dx + AX) * CODE + AY * dy + AY) == code
+                live = jnp.where(hit, column[:, 3:4], live)
+                error = jnp.where(hit, column[:, 2:3], error)
+                value = jnp.where(hit, column[:, 1:2], value)
+                base = jnp.where(hit, column[:, 2:3] + (1.0 - column[:, 3:4]), base)
+            for n, table in enumerate((live, error, value, base)):
+                obs_ref[b, n, :, half * cells : (half + 1) * cells] = table
+
+    scale = 1.0 / (members - 1)
+    gmean, own = moments(own_ref[...], members)
+    own_ref[...] = own
+    alpha, beta = strengths(own, gmean, [obs_ref[0, n, :, :cells] for n in range(4)], members)
+    staged[11].wait()
+    shifted[...] = shift(own, alpha, beta, near_ref[:cells, :])
+    center = (alpha * scale, beta * scale)
+
+    def one_field(v, carry):
+        block = held[v]
+        near = sources_of(shifted, members, around(scale, cells))
+        total, mean = gather(block, [*near, (own_ref[...], *center)])
+        part_ref[v] = block - total
+        fmean[pl.ds(v, 1), :] = fmean[pl.ds(v, 1), :] + mean
+        return carry
+
+    lax.fori_loop(0, fields, one_field, 0)
+    near = sources_of(shifted, members, around(scale, cells))
+    total, mean = gather(own, [*near, (own, *center)])
+    part_ref[fields] = own - total
+    fmean[fields : fields + 1, :] = gmean + mean
+    staged[12].wait()
+    beyond_ref[...] = shift(own, alpha, beta, far_ref[:cells, :])
+
     for cond, copies in sends:
 
         @pl.when(cond)
@@ -319,100 +428,61 @@
                 copy.wait_send()
 
     each(OTHERS, lambda i: remote(i).wait_send())
-    for copy in staged[9:11]:
-        copy.wait()
+    staged[13].wait()
     each(OTHERS, lambda i: border(i).wait_send())
     each(OTHERS, lambda i: border(8 - i).wait_recv())
 
 
 def analysis_kernel(
-    own_ref, halo_ref, metat_ref, fields_in, fmean_ref, code_ref, move_ref,
-    mean_ref, anom_ref,
-    held, shifted, out_sem,
+    own_ref, halo_ref, obs_ref, held_in, part_ref, fmean_ref, beyond_ref, code_ref, near_ref, far_ref, slot_ref,
+    mean_out, anom_ref,
+    held, mean_ref, inner, shifted, out_sem,
 ):
-    fields, members, cells = fields_in.shape
-
+    fields, members, cells = held_in.shape
     scale = 1.0 / (members - 1)
-    grid = jnp.concatenate([own_ref[...], halo_ref[...].T[:members]], axis=1)
-    gmean = jnp.sum(grid, axis=0, keepdims=True) / members
-    grid = grid - gmean
-    code = code_ref[0:1, :]
-
-    for b in range(NB):
-        last = b == NB - 1
-        variance = jnp.sum(grid * grid, axis=0, keepdims=True) / (members - 1)
-        gains = jnp.zeros((OB, 2 * cells), jnp.float32)
-        sums = jnp.zeros((OB, 2 * cells), jnp.float32)
-        weights = jnp.zeros((OB, 2 * cells), jnp.float32)
-        for i in range(9):
-            dx, dy = OFFS[i]
-            column = metat_ref[b * OB : (b + 1) * OB, 8 * i : 8 * i + 4]
-            spot = column[:, 0:1] + float((AX * dx + AX) * CODE + AY * dy + AY)
-            error = column[:, 2:3]
-            live = column[:, 3:4]
-            denom = variance + (error + (1.0 - live))
-            weighting = live / denom
-            damping = 1.0 / (1.0 + jnp.sqrt(error / denom))
-            hit = spot == code
-            weighting = jnp.where(hit, weighting, 0.0)
-            weights = weights + weighting
-            gains = gains + weighting * damping
-            sums = sums + weighting * column[:, 1:2]
-        alpha = jnp.sum(gains, axis=0, keepdims=True)
-        beta = jnp.sum(sums, axis=0, keepdims=True) - gmean * jnp.sum(weights, axis=0, keepdims=True)
-        extra = jnp.concatenate([alpha, beta, jnp.zeros((6, 2 * cells), jnp.float32)], axis=0)
-        left = split_rows(jnp.concatenate([grid, extra], axis=0))
-        width = (8 if last else 16) * cells
-        moved = jnp.dot(left, move_ref[:, :width], preferred_element_type=jnp.float32)
-        rows = members + 8
-        shifted[:, :width] = moved[:rows] + moved[rows:]
-
-        def step(block, part, center, alpha, beta):
-            total = jnp.zeros_like(block)
-            mean = jnp.zeros((1, cells), jnp.float32)
-            for d in range(9):
-                if d == 8:
-                    source, a, m = center, alpha * scale, beta * scale
-                else:
-                    dx, dy = OFFS[OTHERS[d]]
-                    weight = scale * taper_of(dx, dy)
-                    at = (part * 8 + d) * cells
-                    source = shifted[:members, at : at + cells]
-                    a = shifted[members : members + 1, at : at + cells] * weight
-                    m = shifted[members + 1 : members + 2, at : at + cells] * weight
-                cov = jnp.sum(block * source, axis=0, keepdims=True)
-                mean = mean + cov * m
-                total = total + source * (cov * a)
-            return block - total, mean
-
-        own = grid[:, :cells]
-        held[fields] = own
-        own_args = (alpha[:, :cells], beta[:, :cells])
-
-        def one_field(v, carry, own_args=own_args, last=last, b=b, step=step):
-            block, mean = step(fields_in[v] if b == 0 else held[v], 0, held[fields], *own_args)
-            held[v] = block
-            before = fmean_ref[pl.ds(v, 1), :] if b == 0 else mean_ref[v]
-            mean_ref[v] = before + mean
-            if last:
-                pltpu.make_async_copy(held.at[v], anom_ref.at[v], out_sem.at[v]).start()
-            return carry
-
-        lax.fori_loop(0, fields, one_field, 0)
-        block, mean = step(own, 0, own, *own_args)
-        if last:
-            held[fields] = block
-            mean_ref[fields] = gmean[:, :cells] + mean
-            pltpu.make_async_copy(
-                held.at[fields], anom_ref.at[fields], out_sem.at[fields]
-            ).start()
-            for v in range(fields + 1):
-                pltpu.make_async_copy(held.at[v], anom_ref.at[v], out_sem.at[v]).wait()
-        else:
-            outer = grid[:, cells:]
-            far, far_mean = step(outer, 1, outer, alpha[:, cells:], beta[:, cells:])
-            grid = jnp.concatenate([block, far], axis=1)
-            gmean = gmean + jnp.concatenate([mean, far_mean], axis=1)
+    own = own_ref[...]
+    hmean, halo = moments(halo_ref[...].T[:members], members)
+    alpha, beta = strengths(halo, hmean, [obs_ref[0, n, :, cells:] for n in range(4)], members)
+    inner[...] = shift(halo, alpha, beta, slot_ref[cells:, :])
+    taps = [(code_ref[1 + n : 2 + n, :cells] * scale, cells) for n in range(SLOTS)]
+    total, mean = gather(own, sources_of(inner, members, taps))
+    block = part_ref[fields] - total
+    gmean = fmean_ref[fields : fields + 1, :] + mean
+    beyond = beyond_ref[...] + shift(halo, alpha, beta, far_ref[cells:, :])
+    edges = sources_of(beyond, members, around(scale, cells))
+    total, mean = gather(halo, [*edges, (halo, alpha * scale, beta * scale)])
+    grid = jnp.concatenate([block, halo - total], axis=1)
+    gmean = jnp.concatenate([gmean, hmean + mean], axis=1)
+
+    alpha, beta = strengths(grid, gmean, [obs_ref[1, n] for n in range(4)], members)
+    shifted[...] = shift(grid, alpha, beta, near_ref[...])
+    held[fields] = block
+    center = (alpha[:, :cells] * scale, beta[:, :cells] * scale)
+
+    def save(v):
+        return pltpu.make_async_copy(held.at[v], anom_ref.at[v], out_sem.at[v])
+
+    def one_field(v, carry):
+        total, before = gather(held_in[v], sources_of(inner, members, taps))
+        block = part_ref[v] - total
+        near = sources_of(shifted, members, around(scale, cells))
+        total, mean = gather(block, [*near, (held[fields], *center)])
+        held[v] = block - total
+        mean_ref[v] = fmean_ref[pl.ds(v, 1), :] + before + mean
+        save(v).start()
+        return carry
+
+    lax.fori_loop(0, fields, one_field, 0)
+    near = sources_of(shifted, members, around(scale, cells))
+    total, mean = gather(block, [*near, (block, *center)])
+    mean_ref[fields] = gmean[:, :cells] + mean
+    means = pltpu.make_async_copy(mean_ref, mean_out, out_sem.at[fields + 1])
+    means.start()
+    held[fields] = block - total
+    save(fields).start()
+    means.wait()
+    for v in range(fields + 1):
+        save(v).wait()
 
 
 def local(
@@ -424,21 +494,25 @@
     sources, depth = remap_weights.shape[2:4]
     vmem = pl.BlockSpec(memory_space=pltpu.VMEM)
     anywhere = pl.BlockSpec(memory_space=pl.ANY)
-    code, move, out = tables()
+    code, near, far, slot, out = tables()
     results = (
         pltpu.VMEM((members, cells), jnp.float32),
         pltpu.VMEM((cells, 128), jnp.float32),
-        pltpu.VMEM((128, 128), jnp.float32),
+        pltpu.VMEM((NB, 4, OB, 2 * cells), jnp.float32),
         pltpu.VMEM((fields, members, cells), jnp.float32),
-        pltpu.VMEM((fields, cells), jnp.float32),
+        pltpu.VMEM((fields + 1, members, cells), jnp.float32),
+        pltpu.VMEM((16, cells), jnp.float32),
+        pltpu.VMEM((members + 8, 8 * cells), jnp.float32),
         pltpu.VMEM(code.shape, jnp.float32),
-        pltpu.VMEM(move.shape, jnp.bfloat16),
+        pltpu.VMEM(near.shape, jnp.bfloat16),
+        pltpu.VMEM(far.shape, jnp.bfloat16),
+        pltpu.VMEM(slot.shape, jnp.bfloat16),
     )
     state = pl.pallas_call(
         exchange_kernel,
         out_shape=results,
-        in_specs=[anywhere] * 12,
-        out_specs=(vmem,) * 7,
+        in_specs=[anywhere] * 14,
+        out_specs=(vmem,) * len(results),
         scratch_shapes=[
             pltpu.VMEM((9, members, depth), jnp.bfloat16),
             pltpu.VMEM((sources, depth, cells), jnp.bfloat16),
@@ -451,7 +525,8 @@
             pltpu.VMEM((1, slots), jnp.float32),
             pltpu.VMEM(out.shape, jnp.bfloat16),
             pltpu.VMEM((cells, 128), jnp.float32),
-            pltpu.SemaphoreType.DMA((12,)),
+            pltpu.VMEM((members + 8, 8 * cells), jnp.float32),
+            pltpu.SemaphoreType.DMA((14,)),
             pltpu.SemaphoreType.DMA((10, members // PIECE)),
             pltpu.SemaphoreType.DMA((9, members // PIECE)),
             pltpu.SemaphoreType.DMA((4, 9)),
@@ -467,7 +542,7 @@
                 pair_src[0], obs_order[0], obs_cell[0], obs_live[0], obs_value[0], obs_error[0],
                 ocean_members[0, 0], remap_weights[0, 0],
                 jnp.transpose(atm_members[0, 0], (1, 0, 2)),
-                jnp.asarray(code), jnp.asarray(move, jnp.bfloat16), jnp.asarray(out, jnp.bfloat16),
+                jnp.asarray(code), *(jnp.asarray(x, jnp.bfloat16) for x in (near, far, slot, out)),
             )
         )
     )
@@ -477,12 +552,14 @@
             jax.ShapeDtypeStruct((fields + 1, 1, cells), jnp.float32),
             jax.ShapeDtypeStruct((fields + 1, members, cells), jnp.float32),
         ),
-        in_specs=[vmem] * 7,
-        out_specs=(vmem, anywhere),
+        in_specs=[vmem] * len(results),
+        out_specs=(anywhere, anywhere),
         scratch_shapes=[
             pltpu.VMEM((fields + 1, members, cells), jnp.float32),
-            pltpu.VMEM((members + 8, 16 * cells), jnp.float32),
-            pltpu.SemaphoreType.DMA((fields + 1,)),
+            pltpu.VMEM((fields + 1, 1, cells), jnp.float32),
+            pltpu.VMEM((members + 8, SLOTS * cells), jnp.float32),
+            pltpu.VMEM((members + 8, 8 * cells), jnp.float32),
+            pltpu.SemaphoreType.DMA((fields + 2,)),
         ],
         compiler_params=pltpu.CompilerParams(vmem_limit_bytes=LIMIT),
         name="analysis",

time: 21.6 us -> 20 us (0.926)
  Pallas kernels: 20.7 us -> 19.1 us
    pallas_call x1, Pallas kernels: 4.49 us -> 2.82 us  [local(): pl.pallas_call(analysis_kernel, out_shape=(jax.ShapeDtypeStruct((fields +...]
where the time goes in v3:
time: 20 us; the launch traced here: 19.7 us
  Pallas kernels  19.1 us (96%)
  between operations  0.64 us (3%)
    pallas_call x1, Pallas kernels, local(): pl.pallas_call(exchange_kernel, out_shape=results, in_specs=[anywhere] *...  16.2 us
    pallas_call x1, Pallas kernels, local(): pl.pallas_call(analysis_kernel, out_shape=(jax.ShapeDtypeStruct((fields +...  2.82 us

profile of v3, /device:TPU:3, one launch (start us, length us, event | category | flops | bytes accessed | tf_op | source)
XLA Modules:
  0.0 19.7 jit_solution(4649294174077210381)
XLA Ops:
  0.6 16.2 %exchange.1 = (f32[80,128]{1,0:T(8,128)S(1)}, f32[128,128]{1,0:T(8,128)S(1)}, f32[2,4,32,256]{3,2,1,0:T(8,128)S(1)}, f32[12,80,128]{2,1,0:T(8,128)S(1)}, f32[13,...) custom-call(s32[1,4]{1,0:T(1,128)} %bitcast.20, ...), custom_call_target="tpu_custom_call" | custom-call | tf_op jit(solution)/shard_map/exchange/pallas_call | solution.py:511
  16.9 2.8 %analysis.1 = (f32[13,1,128]{2,1,0:T(1,128)}, f32[13,80,128]{2,1,0:T(8,128)}) custom-call(f32[80,128]{1,0:T(8,128)S(1)} %get-tuple-element.15.own_ref, f32[128,128]{1,0:T(8,128)S(1)} %get-tuple-element.16.halo_ref, f32[2,4,32,256]{3,2,1,0:T(8,128)S(1)} %get-tuple-element.17.obs_ref, f32[12,80,128]{2,1,0:T(8,128)S(1)} %get-tuple-element.18.held_in, ...), custom_call_target="tpu_custom_call" | custom-call | tf_op jit(solution)/shard_map/analysis/pallas_call | solution.py:549

commit v4 on v3

--- a/solution.py
+++ b/solution.py
@@ -22,7 +22,8 @@
 NEAR = [1, 3, 5, 7]
 FAR = [0, 2, 6, 8]
 PIECE = 16
-SHARE = 4
+SHARES = (3, 1, 4, 4, 4, 4, 1, 3)
+STEPS = [(True, 4), (True, 3), (False, 0), (False, 1), (True, 2), (False, 2), (True, 1), (False, 3), (True, 0), (False, 4)]
 SLOTS = 5
 
 
@@ -81,7 +82,8 @@
     own = move[:, 0].reshape(2 * cells, 8 * cells)
     far = move[:, 1].reshape(2 * cells, 8 * cells)
     slot = slot.reshape(2 * cells, SLOTS * cells)
-    return code, own, far, slot, out
+    out = np.concatenate([out, np.zeros_like(out)], axis=0)
+    return code, np.concatenate([own, far, slot, out], axis=1)
 
 
 def split_rows(block):
@@ -144,9 +146,9 @@
 
 def exchange_kernel(
     src_ref, order_ref, cell_ref, live_ref, value_ref, error_ref, ocean_ref, weights_ref, atm_ref,
-    code_in, near_in, far_in, slot_in, out_in,
-    own_ref, halo_ref, obs_ref, held, part_ref, fmean, beyond_ref, code_ref, near_ref, far_ref, slot_ref,
-    ocn, wts, meta, src, order_in, cell_in, live_in, value_in, error_in, out, strip_ref, shifted,
+    code_in, table_in,
+    own_ref, halo_ref, obs_ref, held, part_ref, fmean, beyond_ref, code_ref, table_ref,
+    ocn, wts, meta, src, order_in, cell_in, live_in, value_in, error_in, strip_ref, shifted,
     local_sem, send_sem, recv_sem, note_sem,
 ):
     gx, gy = lax.axis_index("gx"), lax.axis_index("gy")
@@ -167,8 +169,7 @@
     pairs = (
         (ocean_ref, ocn.at[4]), (order_ref, order_in), (cell_ref, cell_in), (live_ref, live_in),
         (value_ref, value_in), (error_ref, error_in), (src_ref, src), (weights_ref, wts),
-        (atm_ref, held), (code_in, code_ref), (out_in, out), (near_in, near_ref),
-        (far_in, far_ref), (slot_in, slot_ref),
+        (atm_ref, held), (code_in, code_ref), (table_in, table_ref),
     )
     staged = [pltpu.make_async_copy(x, y, local_sem.at[n]) for n, (x, y) in enumerate(pairs)]
     for copy in staged:
@@ -215,72 +216,103 @@
     outer = lax.rem(gy, 2) * 2 - 1
     count = members // PIECE
 
+    def among(y, wanted):
+        at = lax.rem(y + 8, 8)
+        return sum((at == n).astype(jnp.int32) for n, share in enumerate(SHARES) if wanted(share)) > 0
+
     def relayed(y, p):
-        at = lax.rem(y + 8, 8)
-        return ((at == 2) | (at == 5)) if p >= SHARE else ((at != 1) & (at != 6))
-
-    def ocean(p, source, target, kind, dx, dy, shared=False):
+        return among(y, lambda share: p < share)
+
+    def ocean(low, rows, source, target, kind, index, dx, dy):
         return pltpu.make_async_remote_copy(
-            src_ref=ocn.at[source, pl.ds(p * PIECE, PIECE)],
-            dst_ref=ocn.at[target, pl.ds(p * PIECE, PIECE)],
-            send_sem=send_sem.at[kind, p],
-            recv_sem=recv_sem.at[target, 0 if shared else p],
+            src_ref=ocn.at[source, pl.ds(low, rows)],
+            dst_ref=ocn.at[target, pl.ds(low, rows)],
+            send_sem=send_sem.at[kind],
+            recv_sem=recv_sem.at[index],
             device_id=(gx + dx, gy + dy),
             device_id_type=MESH,
         )
 
-    def arrive(p, at, dx, dy):
-        ocean(p, at, at, 0, dx, dy).wait_recv()
-
-    def arrive_all(at, dx, dy):
-        pltpu.make_async_remote_copy(
-            src_ref=ocn.at[at],
-            dst_ref=ocn.at[at],
-            send_sem=send_sem.at[0, 0],
-            recv_sem=recv_sem.at[at, 0],
-            device_id=(gx + dx, gy + dy),
-            device_id_type=MESH,
-        ).wait_recv()
+    def piece(p, *where):
+        return ocean(p * PIECE, PIECE, *where)
+
+    def arrive(at, index, dx, dy, low=0, rows=members):
+        ocean(low, rows, at, at, 0, index, dx, dy).wait_recv()
+
+    def sent(rows, kind, dx, dy):
+        ocean(0, rows, 4, 4, kind, 0, dx, dy).wait_send()
 
     order = range(count)
-    sends = [
-        (has_y(outer), [ocean(p, 4, 4 - outer, 1, 0, outer) for p in order]),
-        (has_x(-1), [ocean(p, 4, 7, 2, -1, 0) for p in reversed(order)]),
-        (has_x(1), [ocean(p, 4, 1, 3, 1, 0) for p in reversed(order)]),
-        (has_y(-outer), [ocean(p, 4, 4 + outer, 0, 0, -outer, True) for p in order]),
-    ]
-    for cond, copies in sends:
-
+
+    def start(cond, copies):
         @pl.when(cond)
         def _():
             for copy in copies:
                 copy.start()
 
+    def from_side(dx):
+        return count * (dx > 0)
+
+    beside, inside = 2 * count, 3 * count
+
+    def corner(dx, inner):
+        return inside + 1 + 2 * (dx > 0) + inner
+
+    start(has_y(outer), [piece(p, 4, 4 - outer, 0, beside + p, 0, outer) for p in order])
+    for dx in (-1, 1):
+        start(
+            has_x(dx),
+            [piece(p, 4, 4 - 3 * dx, 2 + (dx > 0), from_side(-dx) + p, dx, 0) for p in reversed(order)],
+        )
+    start(has_y(-outer), [piece(p, 4, 4 + outer, 1, inside, 0, -outer) for p in order])
+
     def relay(p, dx):
-        return ocean(p, 4 + outer, 4 - 3 * dx + outer, 4 if dx < 0 else 5, dx, 0, True)
+        return piece(p, 4 + outer, 4 - 3 * dx + outer, 4 + (dx > 0), corner(-dx, 0), dx, 0)
 
     def forward(p, dx):
-        return ocean(p, 4 + 3 * dx, 4 + 3 * dx - outer, 6 if dx < 0 else 7, 0, outer, True)
+        return piece(p, 4 + 3 * dx, 4 + 3 * dx - outer, 6 + (dx > 0), corner(dx, 0), 0, outer)
 
     def hand(p, dx):
-        return ocean(p, 4 + 3 * dx, 4 + 3 * dx + outer, 8 if dx < 0 else 9, 0, -outer, True)
-
-    for p in order:
+        return piece(p, 4 + 3 * dx, 4 + 3 * dx + outer, 8 + (dx > 0), corner(dx, 1), 0, -outer)
+
+    def all_sent():
+        @pl.when(has_y(outer))
+        def _():
+            sent(members, 0, 0, outer)
+
+        @pl.when(has_y(-outer))
+        def _():
+            sent(members, 1, 0, -outer)
+
         for dx in (-1, 1):
-            sends.append((has_x(dx) & has_y(outer) & relayed(gy + outer, p), [relay(p, dx)]))
-            sends.append(
-                (has_x(dx) & has_y(outer) & jnp.logical_not(relayed(gy, p)), [forward(p, dx)])
-            )
-    for dx in (-1, 1):
-        sends.append((has_x(dx) & has_y(-outer), [hand(p, dx) for p in order]))
+
+            @pl.when(has_x(dx))
+            def _():
+                sent(members, 2 + (dx > 0), dx, 0)
+
+            @pl.when(has_x(dx) & has_y(-outer))
+            def _():
+                sent(members, 8 + (dx > 0), 0, -outer)
+
+            for n in sorted(set(SHARES)):
+
+                @pl.when(has_x(dx) & has_y(outer) & among(gy + outer, lambda share: share == n))
+                def _():
+                    if n:
+                        sent(n * PIECE, 4 + (dx > 0), dx, 0)
+
+                @pl.when(has_x(dx) & has_y(outer) & among(gy, lambda share: share == n))
+                def _():
+                    if n < count:
+                        sent((count - n) * PIECE, 6 + (dx > 0), 0, outer)
 
     def remote(i):
         dx, dy = OFFS[i]
         return pltpu.make_async_remote_copy(
             src_ref=meta.at[4],
             dst_ref=meta.at[8 - i],
-            send_sem=note_sem.at[0, i],
-            recv_sem=note_sem.at[1, 8 - i],
+            send_sem=note_sem.at[0],
+            recv_sem=note_sem.at[1],
             device_id=(gx + dx, gy + dy),
             device_id_type=MESH,
         )
@@ -291,10 +323,38 @@
         return pltpu.make_async_remote_copy(
             src_ref=strip_ref.at[pl.ds(source, rows)],
             dst_ref=halo_ref.at[pl.ds(target, rows)],
-            send_sem=note_sem.at[2, i],
-            recv_sem=note_sem.at[3, 8 - i],
+            send_sem=note_sem.at[2],
+            recv_sem=note_sem.at[3],
             device_id=(gx + dx, gy + dy),
             device_id_type=MESH,
+        )
+
+    beside_x = has_x(-1).astype(jnp.int32) + has_x(1).astype(jnp.int32)
+    beside_y = has_y(-1).astype(jnp.int32) + has_y(1).astype(jnp.int32)
+
+    def all_of(act):
+        for nx_ in range(3):
+            for ny_ in range(3):
+                if nx_ + ny_:
+
+                    @pl.when((beside_x == nx_) & (beside_y == ny_))
+                    def _():
+                        act(nx_, ny_)
+
+    def whole_notes(nx_, ny_):
+        n = (nx_ + 1) * (ny_ + 1) - 1
+        return pltpu.make_async_remote_copy(
+            src_ref=meta.at[pl.ds(0, n)], dst_ref=meta.at[pl.ds(0, n)],
+            send_sem=note_sem.at[0], recv_sem=note_sem.at[1],
+            device_id=(gx, gy + outer), device_id_type=MESH,
+        )
+
+    def whole_border(nx_, ny_):
+        rows = nx_ * SPANS[1][1] + ny_ * SPANS[3][1] + nx_ * ny_ * SPANS[0][1]
+        return pltpu.make_async_remote_copy(
+            src_ref=strip_ref.at[pl.ds(0, rows)], dst_ref=halo_ref.at[pl.ds(0, rows)],
+            send_sem=note_sem.at[2], recv_sem=note_sem.at[3],
+            device_id=(gx, gy + outer), device_id_type=MESH,
         )
 
     def each(which, act):
@@ -313,28 +373,25 @@
         fmean[v : v + 1, :] = mean
         held[v] = block - mean
 
-    for p in order:
-        back = count - 1 - p
+    def from_x(p):
         for dx in (-1, 1):
 
             @pl.when(has_x(dx))
             def _():
-                arrive(back, 4 + 3 * dx, dx, 0)
-
-                @pl.when(has_y(outer) & jnp.logical_not(relayed(gy, back)))
+                arrive(4 + 3 * dx, from_side(dx) + p, dx, 0, p * PIECE, PIECE)
+
+                @pl.when(has_y(outer) & jnp.logical_not(relayed(gy, p)))
                 def _():
-                    forward(back, dx).start()
+                    forward(p, dx).start()
 
                 @pl.when(has_y(-outer))
                 def _():
-                    hand(back, dx).start()
-
-        if p == 0:
-            each(FAR, lambda i: remote(i).start())
-
+                    hand(p, dx).start()
+
+    def from_y(p):
         @pl.when(has_y(outer))
         def _():
-            arrive(p, 4 + outer, 0, outer)
+            arrive(4 + outer, beside + p, 0, outer, p * PIECE, PIECE)
 
             @pl.when(relayed(gy + outer, p))
             def _():
@@ -344,21 +401,25 @@
                     def _():
                         relay(p, dx).start()
 
-    each(OTHERS, lambda i: remote(8 - i).wait_recv())
+    for n, (over_x, p) in enumerate(STEPS):
+        (from_x if over_x else from_y)(p)
+        if n == 0:
+            each(FAR, lambda i: remote(i).start())
+
     staged[6].wait()
     staged[7].wait()
     staged[10].wait()
 
     @pl.when(has_y(-outer))
     def _():
-        arrive_all(4 - outer, 0, -outer)
-
-    for dx in (-1, 1):
-        for dy in (-outer, outer):
+        arrive(4 - outer, inside, 0, -outer)
+
+    for inner, dy in ((1, -outer), (0, outer)):
+        for dx in (-1, 1):
 
             @pl.when(has_x(dx) & has_y(dy))
             def _():
-                arrive_all(4 + 3 * dx + dy, dx, 0)
+                arrive(4 + 3 * dx + dy, corner(dx, inner), dx, 0)
 
     total = jnp.zeros(own_ref.shape, jnp.float32)
     for k in range(wts.shape[0]):
@@ -367,14 +428,17 @@
         position = jnp.clip(position, 0, 8)
         total += jnp.dot(ocn[position], wts[k], preferred_element_type=jnp.float32)
     own_ref[...] = total
-    rest = jnp.zeros((out.shape[0] - members, total.shape[1]), jnp.float32)
+    width = strip_ref.shape[0]
+    near, far = slice(0, 8 * width), slice(8 * width, 16 * width)
+    rest = jnp.zeros((width - members, total.shape[1]), jnp.float32)
     picked = lax.dot_general(
-        out[...], split_rows(jnp.concatenate([total, rest], axis=0)), (((1,), (1,)), ((), ())),
+        table_ref[:width, (16 + SLOTS) * width :], split_rows(jnp.concatenate([total, rest], axis=0)), (((1,), (1,)), ((), ())),
         preferred_element_type=jnp.float32,
     )
-    strip_ref[...] = picked[:, : out.shape[0]] + picked[:, out.shape[0] :]
+    strip_ref[...] = picked[:, :width] + picked[:, width:]
     each(FAR + NEAR, lambda i: border(i).start())
 
+    all_of(lambda *n: whole_notes(*n).wait_recv())
     flat = meta[...].reshape(meta.shape[0] * meta.shape[1], meta.shape[2]).T
     cells = total.shape[1]
     staged[9].wait()
@@ -400,41 +464,32 @@
     gmean, own = moments(own_ref[...], members)
     own_ref[...] = own
     alpha, beta = strengths(own, gmean, [obs_ref[0, n, :, :cells] for n in range(4)], members)
-    staged[11].wait()
-    shifted[...] = shift(own, alpha, beta, near_ref[:cells, :])
+    shifted[...] = shift(own, alpha, beta, table_ref[:cells, near])
     center = (alpha * scale, beta * scale)
 
     def one_field(v, carry):
         block = held[v]
-        near = sources_of(shifted, members, around(scale, cells))
-        total, mean = gather(block, [*near, (own_ref[...], *center)])
+        found = sources_of(shifted, members, around(scale, cells))
+        total, mean = gather(block, [*found, (own_ref[...], *center)])
         part_ref[v] = block - total
         fmean[pl.ds(v, 1), :] = fmean[pl.ds(v, 1), :] + mean
         return carry
 
     lax.fori_loop(0, fields, one_field, 0)
-    near = sources_of(shifted, members, around(scale, cells))
-    total, mean = gather(own, [*near, (own, *center)])
+    found = sources_of(shifted, members, around(scale, cells))
+    total, mean = gather(own, [*found, (own, *center)])
     part_ref[fields] = own - total
     fmean[fields : fields + 1, :] = gmean + mean
-    staged[12].wait()
-    beyond_ref[...] = shift(own, alpha, beta, far_ref[:cells, :])
-
-    for cond, copies in sends:
-
-        @pl.when(cond)
-        def _():
-            for copy in copies:
-                copy.wait_send()
-
-    each(OTHERS, lambda i: remote(i).wait_send())
-    staged[13].wait()
-    each(OTHERS, lambda i: border(i).wait_send())
-    each(OTHERS, lambda i: border(8 - i).wait_recv())
+    beyond_ref[...] = shift(own, alpha, beta, table_ref[:cells, far])
+
+    all_sent()
+    all_of(lambda *n: whole_notes(*n).wait_send())
+    all_of(lambda *n: whole_border(*n).wait_send())
+    all_of(lambda *n: whole_border(*n).wait_recv())
 
 
 def analysis_kernel(
-    own_ref, halo_ref, obs_ref, held_in, part_ref, fmean_ref, beyond_ref, code_ref, near_ref, far_ref, slot_ref,
+    own_ref, halo_ref, obs_ref, held_in, part_ref, fmean_ref, beyond_ref, code_ref, table_ref,
     mean_out, anom_ref,
     held, mean_ref, inner, shifted, out_sem,
 ):
@@ -443,24 +498,24 @@
     own = own_ref[...]
     hmean, halo = moments(halo_ref[...].T[:members], members)
     alpha, beta = strengths(halo, hmean, [obs_ref[0, n, :, cells:] for n in range(4)], members)
-    inner[...] = shift(halo, alpha, beta, slot_ref[cells:, :])
+    inner[...] = shift(halo, alpha, beta, table_ref[cells:, 16 * cells : (16 + SLOTS) * cells])
     taps = [(code_ref[1 + n : 2 + n, :cells] * scale, cells) for n in range(SLOTS)]
     total, mean = gather(own, sources_of(inner, members, taps))
     block = part_ref[fields] - total
     gmean = fmean_ref[fields : fields + 1, :] + mean
-    beyond = beyond_ref[...] + shift(halo, alpha, beta, far_ref[cells:, :])
+    beyond = beyond_ref[...] + shift(halo, alpha, beta, table_ref[cells:, 8 * cells : 16 * cells])
     edges = sources_of(beyond, members, around(scale, cells))
     total, mean = gather(halo, [*edges, (halo, alpha * scale, beta * scale)])
     grid = jnp.concatenate([block, halo - total], axis=1)
     gmean = jnp.concatenate([gmean, hmean + mean], axis=1)
 
     alpha, beta = strengths(grid, gmean, [obs_ref[1, n] for n in range(4)], members)
-    shifted[...] = shift(grid, alpha, beta, near_ref[...])
+    shifted[...] = shift(grid, alpha, beta, table_ref[:, : 8 * cells])
     held[fields] = block
     center = (alpha[:, :cells] * scale, beta[:, :cells] * scale)
 
     def save(v):
-        return pltpu.make_async_copy(held.at[v], anom_ref.at[v], out_sem.at[v])
+        return pltpu.make_async_copy(held.at[v], anom_ref.at[v], out_sem.at[0])
 
     def one_field(v, carry):
         total, before = gather(held_in[v], sources_of(inner, members, taps))
@@ -476,13 +531,12 @@
     near = sources_of(shifted, members, around(scale, cells))
     total, mean = gather(block, [*near, (block, *center)])
     mean_ref[fields] = gmean[:, :cells] + mean
-    means = pltpu.make_async_copy(mean_ref, mean_out, out_sem.at[fields + 1])
+    means = pltpu.make_async_copy(mean_ref, mean_out, out_sem.at[1])
     means.start()
     held[fields] = block - total
     save(fields).start()
     means.wait()
-    for v in range(fields + 1):
-        save(v).wait()
+    pltpu.make_async_copy(held, anom_ref, out_sem.at[0]).wait()
 
 
 def local(
@@ -494,7 +548,7 @@
     sources, depth = remap_weights.shape[2:4]
     vmem = pl.BlockSpec(memory_space=pltpu.VMEM)
     anywhere = pl.BlockSpec(memory_space=pl.ANY)
-    code, near, far, slot, out = tables()
+    code, table = tables()
     results = (
         pltpu.VMEM((members, cells), jnp.float32),
         pltpu.VMEM((cells, 128), jnp.float32),
@@ -504,14 +558,12 @@
         pltpu.VMEM((16, cells), jnp.float32),
         pltpu.VMEM((members + 8, 8 * cells), jnp.float32),
         pltpu.VMEM(code.shape, jnp.float32),
-        pltpu.VMEM(near.shape, jnp.bfloat16),
-        pltpu.VMEM(far.shape, jnp.bfloat16),
-        pltpu.VMEM(slot.shape, jnp.bfloat16),
+        pltpu.VMEM(table.shape, jnp.bfloat16),
     )
     state = pl.pallas_call(
         exchange_kernel,
         out_shape=results,
-        in_specs=[anywhere] * 14,
+        in_specs=[anywhere] * 11,
         out_specs=(vmem,) * len(results),
         scratch_shapes=[
             pltpu.VMEM((9, members, depth), jnp.bfloat16),
@@ -523,13 +575,12 @@
             pltpu.VMEM((1, slots), jnp.int32),
             pltpu.VMEM((1, slots), jnp.float32),
             pltpu.VMEM((1, slots), jnp.float32),
-            pltpu.VMEM(out.shape, jnp.bfloat16),
             pltpu.VMEM((cells, 128), jnp.float32),
             pltpu.VMEM((members + 8, 8 * cells), jnp.float32),
-            pltpu.SemaphoreType.DMA((14,)),
-            pltpu.SemaphoreType.DMA((10, members // PIECE)),
-            pltpu.SemaphoreType.DMA((9, members // PIECE)),
-            pltpu.SemaphoreType.DMA((4, 9)),
+            pltpu.SemaphoreType.DMA((11,)),
+            pltpu.SemaphoreType.DMA((10,)),
+            pltpu.SemaphoreType.DMA((3 * (members // PIECE) + 5,)),
+            pltpu.SemaphoreType.DMA((4,)),
         ],
         compiler_params=pltpu.CompilerParams(
             collective_id=0, has_side_effects=True, vmem_limit_bytes=LIMIT
@@ -542,7 +593,7 @@
                 pair_src[0], obs_order[0], obs_cell[0], obs_live[0], obs_value[0], obs_error[0],
                 ocean_members[0, 0], remap_weights[0, 0],
                 jnp.transpose(atm_members[0, 0], (1, 0, 2)),
-                jnp.asarray(code), *(jnp.asarray(x, jnp.bfloat16) for x in (near, far, slot, out)),
+                jnp.asarray(code), jnp.asarray(table, jnp.bfloat16),
             )
         )
     )
@@ -559,7 +610,7 @@
             pltpu.VMEM((fields + 1, 1, cells), jnp.float32),
             pltpu.VMEM((members + 8, SLOTS * cells), jnp.float32),
             pltpu.VMEM((members + 8, 8 * cells), jnp.float32),
-            pltpu.SemaphoreType.DMA((fields + 2,)),
+            pltpu.SemaphoreType.DMA((2,)),
         ],
         compiler_params=pltpu.CompilerParams(vmem_limit_bytes=LIMIT),
         name="analysis",

time: 20 us -> 18.9 us (0.945)
  Pallas kernels: 19.1 us -> 18.1 us
    pallas_call x1, Pallas kernels: 16.2 us -> 15.3 us  [local(): pl.pallas_call(exchange_kernel, out_shape=results, in_specs=[anywhere] *...]
where the time goes in v4:
time: 18.9 us; the launch traced here: 18.7 us
  Pallas kernels  18.1 us (96%)
  between operations  0.64 us (3%)
    pallas_call x1, Pallas kernels, local(): pl.pallas_call(exchange_kernel, out_shape=results, in_specs=[anywhere] *...  15.3 us
    pallas_call x1, Pallas kernels, local(): pl.pallas_call(analysis_kernel, out_shape=(jax.ShapeDtypeStruct((fields +...  2.73 us

profile of v4, /device:TPU:3, one launch (start us, length us, event | category | flops | bytes accessed | tf_op | source)
XLA Modules:
  0.0 18.7 jit_solution(8019516574682768472)
XLA Ops:
  0.6 15.3 %exchange.1 = (f32[80,128]{1,0:T(8,128)S(1)}, f32[128,128]{1,0:T(8,128)S(1)}, f32[2,4,32,256]{3,2,1,0:T(8,128)S(1)}, f32[12,80,128]{2,1,0:T(8,128)S(1)}, f32[13,...) custom-call(s32[1,4]{1,0:T(1,128)} %bitcast.20, ...), custom_call_target="tpu_custom_call" | custom-call | tf_op jit(solution)/shard_map/exchange/pallas_call | solution.py:563
  16.0 2.7 %analysis.1 = (f32[13,1,128]{2,1,0:T(1,128)}, f32[13,80,128]{2,1,0:T(8,128)}) custom-call(f32[80,128]{1,0:T(8,128)S(1)} %get-tuple-element.13.own_ref, f32[128,128]{1,0:T(8,128)S(1)} %get-tuple-element.14.halo_ref, f32[2,4,32,256]{3,2,1,0:T(8,128)S(1)} %get-tuple-element.15.obs_ref, f32[12,80,128]{2,1,0:T(8,128)S(1)} %get-tuple-element.16.held_in, ...), custom_call_target="tpu_custom_call" | custom-call | tf_op jit(solution)/shard_map/analysis/pallas_call | solution.py:600

commit v5 on v4

--- a/solution.py
+++ b/solution.py
@@ -22,8 +22,9 @@
 NEAR = [1, 3, 5, 7]
 FAR = [0, 2, 6, 8]
 PIECE = 16
-SHARES = (3, 1, 4, 4, 4, 4, 1, 3)
-STEPS = [(True, 4), (True, 3), (False, 0), (False, 1), (True, 2), (False, 2), (True, 1), (False, 3), (True, 0), (False, 4)]
+SHARES = (3, 1, 3, 4, 4, 3, 1, 3)
+EVEN = [(False, 0), (False, 1), (True, 4), (False, 2), (True, 3), (True, 2), (False, 3), (True, 1), (True, 0), (False, 4)]
+ODD = [(True, 4), (True, 3), (False, 0), (True, 2), (False, 1), (True, 1), (False, 2), (True, 0), (False, 3), (False, 4)]
 SLOTS = 5
 
 
@@ -63,12 +64,12 @@
             out[SPANS[i][0] + n, x * AY + y] = 1.0
         for n, (x, y) in enumerate(strip(8 - i)):
             where[(x + dx * AX, y + dy * AY)] = cells + SPANS[i][0] + n
-    code = np.full((8, 2 * cells), -1.0, np.float32)
-    code[1:, :] = 0.0
+    code = np.zeros((2 * cells, 2 * cells), np.float32)
+    code[:2, :] = -1.0
     move = np.zeros((2 * cells, 2, 8, cells), np.float32)
     slot = np.zeros((2 * cells, SLOTS, cells), np.float32)
     for (x, y), n in where.items():
-        code[0, n] = (x + AX) * CODE + (y + AY)
+        code[0, n], code[1, n] = x + AX, y + AY
         taken = 0
         for d, i in enumerate(OTHERS):
             dx, dy = OFFS[i]
@@ -77,13 +78,13 @@
                 move[src, n // cells, d, n % cells] = 1.0
                 if n < cells <= src:
                     slot[src, taken, n] = 1.0
-                    code[1 + taken, n] = taper_of(dx, dy)
+                    code[2 + taken, n] = taper_of(dx, dy)
                     taken += 1
     own = move[:, 0].reshape(2 * cells, 8 * cells)
     far = move[:, 1].reshape(2 * cells, 8 * cells)
     slot = slot.reshape(2 * cells, SLOTS * cells)
     out = np.concatenate([out, np.zeros_like(out)], axis=0)
-    return code, np.concatenate([own, far, slot, out], axis=1)
+    return np.concatenate([own, far, slot, out, code], axis=1)
 
 
 def split_rows(block):
@@ -146,16 +147,16 @@
 
 def exchange_kernel(
     src_ref, order_ref, cell_ref, live_ref, value_ref, error_ref, ocean_ref, weights_ref, atm_ref,
-    code_in, table_in,
-    own_ref, halo_ref, obs_ref, held, part_ref, fmean, beyond_ref, code_ref, table_ref,
-    ocn, wts, meta, src, order_in, cell_in, live_in, value_in, error_in, strip_ref, shifted,
+    table_in,
+    own_ref, halo_ref, obs_ref, held, part_ref, fmean, beyond_ref, table_ref,
+    ocn, late, wts, meta, src, ints, floats, strip_ref, shifted,
     local_sem, send_sem, recv_sem, note_sem,
 ):
     gx, gy = lax.axis_index("gx"), lax.axis_index("gy")
     nx, ny = lax.axis_size("gx"), lax.axis_size("gy")
     members = own_ref.shape[0]
     fields = atm_ref.shape[0]
-    slots = order_in.shape[1]
+    slots = ints.shape[2]
 
     def has_x(dx):
         return (gx + dx >= 0) & (gx + dx < nx)
@@ -166,12 +167,15 @@
     def there(i):
         return has_x(OFFS[i][0]) & has_y(OFFS[i][1])
 
+    depth = wts.shape[0] - 1
     pairs = (
-        (ocean_ref, ocn.at[4]), (order_ref, order_in), (cell_ref, cell_in), (live_ref, live_in),
-        (value_ref, value_in), (error_ref, error_in), (src_ref, src), (weights_ref, wts),
-        (atm_ref, held), (code_in, code_ref), (table_in, table_ref),
+        (ocean_ref, ocn.at[4], 0), (order_ref, ints.at[0], 1), (cell_ref, ints.at[1], 1),
+        (live_ref, ints.at[2], 1), (value_ref, floats.at[0], 2), (error_ref, floats.at[1], 2),
+        (src_ref, src, 3), (weights_ref, wts.at[0:depth], 4), (atm_ref, held, 5),
+        (table_in, table_ref, 6),
     )
-    staged = [pltpu.make_async_copy(x, y, local_sem.at[n]) for n, (x, y) in enumerate(pairs)]
+    staged = [pltpu.make_async_copy(x, y, local_sem.at[n]) for x, y, n in pairs]
+    outer = lax.rem(gy, 2) * 2 - 1
     for copy in staged:
         copy.start()
 
@@ -191,29 +195,20 @@
             halo_ref[at : at + rows, :] = jnp.zeros((rows, halo_ref.shape[1]), jnp.float32)
             meta[i] = jnp.zeros(meta.shape[1:], jnp.float32)
 
+    for dx in (-1, 1):
+        ocn[4 + 3 * dx + outer] = jnp.zeros(ocn.shape[1:], ocn.dtype)
+
+        @pl.when(jnp.logical_not(has_x(dx) & has_y(outer)))
+        def _():
+            late[int(dx > 0)] = jnp.zeros(late.shape[1:], late.dtype)
+
+    wts[depth] = jnp.zeros(wts.shape[1:], wts.dtype)
     for n in range(9, meta.shape[0]):
         meta[n] = jnp.zeros(meta.shape[1:], jnp.float32)
 
-    for copy in staged[1:6]:
-        copy.wait()
-    cell = cell_in[...]
-    spot = ((cell // AY) * CODE + cell % AY).astype(jnp.float32)
-    rows = jnp.concatenate(
-        [
-            spot, value_in[...], error_in[...], live_in[...].astype(jnp.float32),
-            jnp.zeros((4, slots), jnp.float32),
-        ],
-        axis=0,
-    )
-    slot = lax.broadcasted_iota(jnp.int32, (slots, slots), 0)
-    perm = jnp.where(order_in[...] == slot, 1.0, 0.0)
-    rows = jnp.dot(rows, perm, precision=lax.Precision.HIGHEST, preferred_element_type=jnp.float32)
-    meta[4] = jnp.concatenate([rows, jnp.zeros((8, meta.shape[2] - slots), jnp.float32)], axis=1)
-
     staged[0].wait()
     pl.semaphore_wait(barrier, sum(there(i).astype(jnp.int32) for i in NEAR))
 
-    outer = lax.rem(gy, 2) * 2 - 1
     count = members // PIECE
 
     def among(y, wanted):
@@ -226,21 +221,31 @@
     def ocean(low, rows, source, target, kind, index, dx, dy):
         return pltpu.make_async_remote_copy(
             src_ref=ocn.at[source, pl.ds(low, rows)],
-            dst_ref=ocn.at[target, pl.ds(low, rows)],
-            send_sem=send_sem.at[kind],
+            dst_ref=target.at[pl.ds(low, rows)],
+            send_sem=send_sem.at[0],
             recv_sem=recv_sem.at[index],
             device_id=(gx + dx, gy + dy),
             device_id_type=MESH,
         )
 
-    def piece(p, *where):
-        return ocean(p * PIECE, PIECE, *where)
-
-    def arrive(at, index, dx, dy, low=0, rows=members):
-        ocean(low, rows, at, at, 0, index, dx, dy).wait_recv()
+    def piece(p, source, target, kind, index, dx, dy):
+        return ocean(p * PIECE, PIECE, source, target, kind, index, dx, dy)
+
+    def arrive(at, index, dx, dy, p):
+        ocean(p * PIECE, PIECE, at, ocn.at[at], 0, index, dx, dy).wait_recv()
 
     def sent(rows, kind, dx, dy):
-        ocean(0, rows, 4, 4, kind, 0, dx, dy).wait_send()
+        ocean(0, rows, 4, ocn.at[4], kind, 0, dx, dy).wait_send()
+
+    def whole(blocks, index, dx, dy):
+        pltpu.make_async_remote_copy(
+            src_ref=ocn.at[pl.ds(0, blocks)],
+            dst_ref=ocn.at[pl.ds(0, blocks)],
+            send_sem=send_sem.at[0],
+            recv_sem=recv_sem.at[index],
+            device_id=(gx + dx, gy + dy),
+            device_id_type=MESH,
+        ).wait_recv()
 
     order = range(count)
 
@@ -255,25 +260,28 @@
 
     beside, inside = 2 * count, 3 * count
 
-    def corner(dx, inner):
-        return inside + 1 + 2 * (dx > 0) + inner
-
-    start(has_y(outer), [piece(p, 4, 4 - outer, 0, beside + p, 0, outer) for p in order])
+    mine = lax.rem(gy, 8)
+    yields = (mine == 2) | (mine == 5)
+    to_outer = [piece(p, 4, ocn.at[4 - outer], 0, beside + p, 0, outer) for p in order]
+    start(has_y(outer) & jnp.logical_not(yields), to_outer)
     for dx in (-1, 1):
         start(
             has_x(dx),
-            [piece(p, 4, 4 - 3 * dx, 2 + (dx > 0), from_side(-dx) + p, dx, 0) for p in reversed(order)],
-        )
-    start(has_y(-outer), [piece(p, 4, 4 + outer, 1, inside, 0, -outer) for p in order])
+            [
+                piece(p, 4, ocn.at[4 - 3 * dx], 2 + (dx > 0), from_side(-dx) + p, dx, 0)
+                for p in reversed(order)
+            ],
+        )
+    start(has_y(-outer), [ocean(0, members, 4, ocn.at[4 + outer], 1, inside, 0, -outer)])
 
     def relay(p, dx):
-        return piece(p, 4 + outer, 4 - 3 * dx + outer, 4 + (dx > 0), corner(-dx, 0), dx, 0)
+        return piece(p, 4 + outer, late.at[int(dx < 0)], 4 + (dx > 0), inside + 1, dx, 0)
 
     def forward(p, dx):
-        return piece(p, 4 + 3 * dx, 4 + 3 * dx - outer, 6 + (dx > 0), corner(dx, 0), 0, outer)
+        return piece(p, 4 + 3 * dx, late.at[int(dx > 0)], 6 + (dx > 0), inside + 1, 0, outer)
 
     def hand(p, dx):
-        return piece(p, 4 + 3 * dx, 4 + 3 * dx + outer, 8 + (dx > 0), corner(dx, 1), 0, -outer)
+        return piece(p, 4 + 3 * dx, ocn.at[4 + 3 * dx + outer], 8 + (dx > 0), inside, 0, -outer)
 
     def all_sent():
         @pl.when(has_y(outer))
@@ -305,14 +313,17 @@
                 def _():
                     if n < count:
                         sent((count - n) * PIECE, 6 + (dx > 0), 0, outer)
+
+    beside_x = has_x(-1).astype(jnp.int32) + has_x(1).astype(jnp.int32)
+    beside_y = has_y(-1).astype(jnp.int32) + has_y(1).astype(jnp.int32)
 
     def remote(i):
         dx, dy = OFFS[i]
         return pltpu.make_async_remote_copy(
             src_ref=meta.at[4],
             dst_ref=meta.at[8 - i],
-            send_sem=note_sem.at[0],
-            recv_sem=note_sem.at[1],
+            send_sem=send_sem.at[0],
+            recv_sem=note_sem.at[0],
             device_id=(gx + dx, gy + dy),
             device_id_type=MESH,
         )
@@ -323,14 +334,11 @@
         return pltpu.make_async_remote_copy(
             src_ref=strip_ref.at[pl.ds(source, rows)],
             dst_ref=halo_ref.at[pl.ds(target, rows)],
-            send_sem=note_sem.at[2],
-            recv_sem=note_sem.at[3],
+            send_sem=send_sem.at[0],
+            recv_sem=note_sem.at[1],
             device_id=(gx + dx, gy + dy),
             device_id_type=MESH,
         )
-
-    beside_x = has_x(-1).astype(jnp.int32) + has_x(1).astype(jnp.int32)
-    beside_y = has_y(-1).astype(jnp.int32) + has_y(1).astype(jnp.int32)
 
     def all_of(act):
         for nx_ in range(3):
@@ -345,7 +353,7 @@
         n = (nx_ + 1) * (ny_ + 1) - 1
         return pltpu.make_async_remote_copy(
             src_ref=meta.at[pl.ds(0, n)], dst_ref=meta.at[pl.ds(0, n)],
-            send_sem=note_sem.at[0], recv_sem=note_sem.at[1],
+            send_sem=send_sem.at[0], recv_sem=note_sem.at[0],
             device_id=(gx, gy + outer), device_id_type=MESH,
         )
 
@@ -353,7 +361,7 @@
         rows = nx_ * SPANS[1][1] + ny_ * SPANS[3][1] + nx_ * ny_ * SPANS[0][1]
         return pltpu.make_async_remote_copy(
             src_ref=strip_ref.at[pl.ds(0, rows)], dst_ref=halo_ref.at[pl.ds(0, rows)],
-            send_sem=note_sem.at[2], recv_sem=note_sem.at[3],
+            send_sem=send_sem.at[0], recv_sem=note_sem.at[1],
             device_id=(gx, gy + outer), device_id_type=MESH,
         )
 
@@ -363,6 +371,22 @@
             @pl.when(there(i))
             def _():
                 act(i)
+
+    pltpu.make_async_copy(ints, ints, local_sem.at[1]).wait()
+    pltpu.make_async_copy(floats, floats, local_sem.at[2]).wait()
+    cell = ints[1]
+    spot = ((cell // AY) * CODE + cell % AY).astype(jnp.float32)
+    rows = jnp.concatenate(
+        [
+            spot, floats[0], floats[1], ints[2].astype(jnp.float32),
+            jnp.zeros((4, slots), jnp.float32),
+        ],
+        axis=0,
+    )
+    slot = lax.broadcasted_iota(jnp.int32, (slots, slots), 0)
+    perm = jnp.where(ints[0] == slot, 1.0, 0.0)
+    rows = jnp.dot(rows, perm, precision=lax.Precision.HIGHEST, preferred_element_type=jnp.float32)
+    meta[4] = jnp.concatenate([rows, jnp.zeros((8, meta.shape[2] - slots), jnp.float32)], axis=1)
 
     each(NEAR, lambda i: remote(i).start())
 
@@ -373,12 +397,14 @@
         fmean[v : v + 1, :] = mean
         held[v] = block - mean
 
+    start(has_y(outer) & yields, to_outer)
+
     def from_x(p):
         for dx in (-1, 1):
 
             @pl.when(has_x(dx))
             def _():
-                arrive(4 + 3 * dx, from_side(dx) + p, dx, 0, p * PIECE, PIECE)
+                arrive(4 + 3 * dx, from_side(dx) + p, dx, 0, p)
 
                 @pl.when(has_y(outer) & jnp.logical_not(relayed(gy, p)))
                 def _():
@@ -391,7 +417,7 @@
     def from_y(p):
         @pl.when(has_y(outer))
         def _():
-            arrive(4 + outer, beside + p, 0, outer, p * PIECE, PIECE)
+            arrive(4 + outer, beside + p, 0, outer, p)
 
             @pl.when(relayed(gy + outer, p))
             def _():
@@ -401,38 +427,56 @@
                     def _():
                         relay(p, dx).start()
 
-    for n, (over_x, p) in enumerate(STEPS):
-        (from_x if over_x else from_y)(p)
-        if n == 0:
-            each(FAR, lambda i: remote(i).start())
+    for parity, steps in enumerate((EVEN, ODD)):
+
+        @pl.when(lax.rem(gy, 2) == parity)
+        def _():
+            first = [over_x for over_x, _ in steps].index(True)
+            for n, (over_x, p) in enumerate(steps):
+                (from_x if over_x else from_y)(p)
+                if n == first:
+                    each(FAR, lambda i: remote(i).start())
 
     staged[6].wait()
     staged[7].wait()
-    staged[10].wait()
-
-    @pl.when(has_y(-outer))
-    def _():
-        arrive(4 - outer, inside, 0, -outer)
-
-    for inner, dy in ((1, -outer), (0, outer)):
-        for dx in (-1, 1):
-
-            @pl.when(has_x(dx) & has_y(dy))
-            def _():
-                arrive(4 + 3 * dx + dy, corner(dx, inner), dx, 0)
+    staged[9].wait()
+    for n in range(3):
+
+        @pl.when((beside_x == n) & has_y(-outer))
+        def _():
+            whole(n + 1, inside, 0, -outer)
 
     total = jnp.zeros(own_ref.shape, jnp.float32)
-    for k in range(wts.shape[0]):
+    places = []
+    for k in range(depth):
         source = src[0, k]
         position = (source // ny - gx + 1) * 3 + (source % ny - gy + 1)
-        position = jnp.clip(position, 0, 8)
-        total += jnp.dot(ocn[position], wts[k], preferred_element_type=jnp.float32)
+        places.append(jnp.clip(position, 0, 8))
+        total += jnp.dot(ocn[places[k]], wts[k], preferred_element_type=jnp.float32)
     own_ref[...] = total
+
+    @pl.when(has_y(outer))
+    def _():
+        for n in range(1, 3):
+
+            @pl.when(beside_x == n)
+            def _():
+                whole(n, inside + 1, 0, outer)
+
+        total = own_ref[...]
+        for dx in (-1, 1):
+            match = depth
+            for k in range(depth):
+                match = jnp.where(places[k] == 4 + 3 * dx + outer, k, match)
+            total += jnp.dot(late[int(dx > 0)], wts[match], preferred_element_type=jnp.float32)
+        own_ref[...] = total
+
+    total = own_ref[...]
     width = strip_ref.shape[0]
     near, far = slice(0, 8 * width), slice(8 * width, 16 * width)
     rest = jnp.zeros((width - members, total.shape[1]), jnp.float32)
     picked = lax.dot_general(
-        table_ref[:width, (16 + SLOTS) * width :], split_rows(jnp.concatenate([total, rest], axis=0)), (((1,), (1,)), ((), ())),
+        table_ref[:width, (16 + SLOTS) * width : (17 + SLOTS) * width], split_rows(jnp.concatenate([total, rest], axis=0)), (((1,), (1,)), ((), ())),
         preferred_element_type=jnp.float32,
     )
     strip_ref[...] = picked[:, :width] + picked[:, width:]
@@ -441,10 +485,11 @@
     all_of(lambda *n: whole_notes(*n).wait_recv())
     flat = meta[...].reshape(meta.shape[0] * meta.shape[1], meta.shape[2]).T
     cells = total.shape[1]
-    staged[9].wait()
+    places = table_ref[:16, (17 + SLOTS) * cells :].astype(jnp.float32)
+    places = places[0:1] * CODE + places[1:2]
     for b in range(NB):
         for half, tiles in ((0, [4]), (1, OTHERS)):
-            code = code_ref[0:1, half * cells : (half + 1) * cells]
+            code = places[:, half * cells : (half + 1) * cells]
             live = jnp.zeros((OB, cells), jnp.float32)
             error = live + 1.0
             value = live
@@ -489,7 +534,7 @@
 
 
 def analysis_kernel(
-    own_ref, halo_ref, obs_ref, held_in, part_ref, fmean_ref, beyond_ref, code_ref, table_ref,
+    own_ref, halo_ref, obs_ref, held_in, part_ref, fmean_ref, beyond_ref, table_ref,
     mean_out, anom_ref,
     held, mean_ref, inner, shifted, out_sem,
 ):
@@ -499,7 +544,8 @@
     hmean, halo = moments(halo_ref[...].T[:members], members)
     alpha, beta = strengths(halo, hmean, [obs_ref[0, n, :, cells:] for n in range(4)], members)
     inner[...] = shift(halo, alpha, beta, table_ref[cells:, 16 * cells : (16 + SLOTS) * cells])
-    taps = [(code_ref[1 + n : 2 + n, :cells] * scale, cells) for n in range(SLOTS)]
+    taps = table_ref[:16, (17 + SLOTS) * cells : (18 + SLOTS) * cells].astype(jnp.float32) * scale
+    taps = [(taps[2 + n : 3 + n], cells) for n in range(SLOTS)]
     total, mean = gather(own, sources_of(inner, members, taps))
     block = part_ref[fields] - total
     gmean = fmean_ref[fields : fields + 1, :] + mean
@@ -548,7 +594,7 @@
     sources, depth = remap_weights.shape[2:4]
     vmem = pl.BlockSpec(memory_space=pltpu.VMEM)
     anywhere = pl.BlockSpec(memory_space=pl.ANY)
-    code, table = tables()
+    table = tables()
     results = (
         pltpu.VMEM((members, cells), jnp.float32),
         pltpu.VMEM((cells, 128), jnp.float32),
@@ -557,30 +603,27 @@
         pltpu.VMEM((fields + 1, members, cells), jnp.float32),
         pltpu.VMEM((16, cells), jnp.float32),
         pltpu.VMEM((members + 8, 8 * cells), jnp.float32),
-        pltpu.VMEM(code.shape, jnp.float32),
         pltpu.VMEM(table.shape, jnp.bfloat16),
     )
     state = pl.pallas_call(
         exchange_kernel,
         out_shape=results,
-        in_specs=[anywhere] * 11,
+        in_specs=[anywhere] * 10,
         out_specs=(vmem,) * len(results),
         scratch_shapes=[
             pltpu.VMEM((9, members, depth), jnp.bfloat16),
-            pltpu.VMEM((sources, depth, cells), jnp.bfloat16),
+            pltpu.VMEM((2, members, depth), jnp.bfloat16),
+            pltpu.VMEM((sources + 1, depth, cells), jnp.bfloat16),
             pltpu.VMEM((16, 8, 128), jnp.float32),
             pltpu.SMEM((1, sources), jnp.int32),
-            pltpu.VMEM((1, slots), jnp.int32),
-            pltpu.VMEM((1, slots), jnp.int32),
-            pltpu.VMEM((1, slots), jnp.int32),
-            pltpu.VMEM((1, slots), jnp.float32),
-            pltpu.VMEM((1, slots), jnp.float32),
+            pltpu.VMEM((3, 1, slots), jnp.int32),
+            pltpu.VMEM((2, 1, slots), jnp.float32),
             pltpu.VMEM((cells, 128), jnp.float32),
             pltpu.VMEM((members + 8, 8 * cells), jnp.float32),
-            pltpu.SemaphoreType.DMA((11,)),
-            pltpu.SemaphoreType.DMA((10,)),
-            pltpu.SemaphoreType.DMA((3 * (members // PIECE) + 5,)),
-            pltpu.SemaphoreType.DMA((4,)),
+            pltpu.SemaphoreType.DMA((7,)),
+            pltpu.SemaphoreType.DMA((1,)),
+            pltpu.SemaphoreType.DMA((3 * (members // PIECE) + 2,)),
+            pltpu.SemaphoreType.DMA((2,)),
         ],
         compiler_params=pltpu.CompilerParams(
             collective_id=0, has_side_effects=True, vmem_limit_bytes=LIMIT
@@ -593,7 +636,7 @@
                 pair_src[0], obs_order[0], obs_cell[0], obs_live[0], obs_value[0], obs_error[0],
                 ocean_members[0, 0], remap_weights[0, 0],
                 jnp.transpose(atm_members[0, 0], (1, 0, 2)),
-                jnp.asarray(code), jnp.asarray(table, jnp.bfloat16),
+                jnp.asarray(table, jnp.bfloat16),
             )
         )
     )

time: 18.9 us -> 18 us (0.952)
  Pallas kernels: 18.1 us -> 17.1 us
    pallas_call x1, Pallas kernels: 15.3 us -> 14.3 us  [local(): pl.pallas_call(exchange_kernel, out_shape=results, in_specs=[anywhere] *...]
where the time goes in v5:
time: 18 us; the launch traced here: 17.7 us
  Pallas kernels  17.1 us (95%)
  between operations  0.64 us (4%)
    pallas_call x1, Pallas kernels, local(): pl.pallas_call(exchange_kernel, out_shape=results, in_specs=[anywhere] *...  14.3 us
    pallas_call x1, Pallas kernels, local(): pl.pallas_call(analysis_kernel, out_shape=(jax.ShapeDtypeStruct((fields +...  2.73 us

profile of v5, /device:TPU:3, one launch (start us, length us, event | category | flops | bytes accessed | tf_op | source)
XLA Modules:
  0.0 17.7 jit_solution(3119534103803087923)
XLA Ops:
  0.6 14.3 %exchange.1 = (f32[80,128]{1,0:T(8,128)S(1)}, f32[128,128]{1,0:T(8,128)S(1)}, f32[2,4,32,256]{3,2,1,0:T(8,128)S(1)}, f32[12,80,128]{2,1,0:T(8,128)S(1)}, f32[13,...) custom-call(s32[1,4]{1,0:T(1,128)} %bitcast.20, ...), custom_call_target="tpu_custom_call" | custom-call | tf_op jit(solution)/shard_map/exchange/pallas_call | solution.py:608
  15.0 2.7 %analysis.1 = (f32[13,1,128]{2,1,0:T(1,128)}, f32[13,80,128]{2,1,0:T(8,128)}) custom-call(f32[80,128]{1,0:T(8,128)S(1)} %get-tuple-element.12.own_ref, f32[128,128]{1,0:T(8,128)S(1)} %get-tuple-element.13.halo_ref, f32[2,4,32,256]{3,2,1,0:T(8,128)S(1)} %get-tuple-element.14.obs_ref, f32[12,80,128]{2,1,0:T(8,128)S(1)} %get-tuple-element.15.held_in, ...), custom_call_target="tpu_custom_call" | custom-call | tf_op jit(solution)/shard_map/analysis/pallas_call | solution.py:643

commit v6 on v5

--- a/solution.py
+++ b/solution.py
@@ -116,14 +116,13 @@
     return moved[:rows] + moved[rows:]
 
 
-def gather(block, sources):
-    total = jnp.zeros_like(block)
+def gather(block, sources, left):
     mean = jnp.zeros((1, block.shape[1]), jnp.float32)
     for source, a, m in sources:
         cov = jnp.sum(block * source, axis=0, keepdims=True)
         mean = mean + cov * m
-        total = total + source * (cov * a)
-    return total, mean
+        left = left - source * (cov * a)
+    return left, mean
 
 
 def sources_of(shifted, members, weights):
@@ -167,6 +166,14 @@
     def there(i):
         return has_x(OFFS[i][0]) & has_y(OFFS[i][1])
 
+    barrier = pltpu.get_barrier_semaphore()
+    for i in NEAR:
+        dx, dy = OFFS[i]
+
+        @pl.when(there(i))
+        def _():
+            pl.semaphore_signal(barrier, inc=1, device_id=(gx + dx, gy + dy), device_id_type=MESH)
+
     depth = wts.shape[0] - 1
     pairs = (
         (ocean_ref, ocn.at[4], 0), (order_ref, ints.at[0], 1), (cell_ref, ints.at[1], 1),
@@ -178,14 +185,6 @@
     outer = lax.rem(gy, 2) * 2 - 1
     for copy in staged:
         copy.start()
-
-    barrier = pltpu.get_barrier_semaphore()
-    for i in NEAR:
-        dx, dy = OFFS[i]
-
-        @pl.when(there(i))
-        def _():
-            pl.semaphore_signal(barrier, inc=1, device_id=(gx + dx, gy + dy), device_id_type=MESH)
 
     for i in OTHERS:
 
@@ -453,25 +452,18 @@
         position = (source // ny - gx + 1) * 3 + (source % ny - gy + 1)
         places.append(jnp.clip(position, 0, 8))
         total += jnp.dot(ocn[places[k]], wts[k], preferred_element_type=jnp.float32)
+    for n in range(1, 3):
+
+        @pl.when((beside_x == n) & has_y(outer))
+        def _():
+            whole(n, inside + 1, 0, outer)
+
+    for dx in (-1, 1):
+        match = depth
+        for k in range(depth):
+            match = jnp.where(places[k] == 4 + 3 * dx + outer, k, match)
+        total += jnp.dot(late[int(dx > 0)], wts[match], preferred_element_type=jnp.float32)
     own_ref[...] = total
-
-    @pl.when(has_y(outer))
-    def _():
-        for n in range(1, 3):
-
-            @pl.when(beside_x == n)
-            def _():
-                whole(n, inside + 1, 0, outer)
-
-        total = own_ref[...]
-        for dx in (-1, 1):
-            match = depth
-            for k in range(depth):
-                match = jnp.where(places[k] == 4 + 3 * dx + outer, k, match)
-            total += jnp.dot(late[int(dx > 0)], wts[match], preferred_element_type=jnp.float32)
-        own_ref[...] = total
-
-    total = own_ref[...]
     width = strip_ref.shape[0]
     near, far = slice(0, 8 * width), slice(8 * width, 16 * width)
     rest = jnp.zeros((width - members, total.shape[1]), jnp.float32)
@@ -515,15 +507,13 @@
     def one_field(v, carry):
         block = held[v]
         found = sources_of(shifted, members, around(scale, cells))
-        total, mean = gather(block, [*found, (own_ref[...], *center)])
-        part_ref[v] = block - total
+        part_ref[v], mean = gather(block, [*found, (own_ref[...], *center)], block)
         fmean[pl.ds(v, 1), :] = fmean[pl.ds(v, 1), :] + mean
         return carry
 
     lax.fori_loop(0, fields, one_field, 0)
     found = sources_of(shifted, members, around(scale, cells))
-    total, mean = gather(own, [*found, (own, *center)])
-    part_ref[fields] = own - total
+    part_ref[fields], mean = gather(own, [*found, (own, *center)], own)
     fmean[fields : fields + 1, :] = gmean + mean
     beyond_ref[...] = shift(own, alpha, beta, table_ref[:cells, far])
 
@@ -546,13 +536,12 @@
     inner[...] = shift(halo, alpha, beta, table_ref[cells:, 16 * cells : (16 + SLOTS) * cells])
     taps = table_ref[:16, (17 + SLOTS) * cells : (18 + SLOTS) * cells].astype(jnp.float32) * scale
     taps = [(taps[2 + n : 3 + n], cells) for n in range(SLOTS)]
-    total, mean = gather(own, sources_of(inner, members, taps))
-    block = part_ref[fields] - total
+    block, mean = gather(own, sources_of(inner, members, taps), part_ref[fields])
     gmean = fmean_ref[fields : fields + 1, :] + mean
     beyond = beyond_ref[...] + shift(halo, alpha, beta, table_ref[cells:, 8 * cells : 16 * cells])
     edges = sources_of(beyond, members, around(scale, cells))
-    total, mean = gather(halo, [*edges, (halo, alpha * scale, beta * scale)])
-    grid = jnp.concatenate([block, halo - total], axis=1)
+    halo, mean = gather(halo, [*edges, (halo, alpha * scale, beta * scale)], halo)
+    grid = jnp.concatenate([block, halo], axis=1)
     gmean = jnp.concatenate([gmean, hmean + mean], axis=1)
 
     alpha, beta = strengths(grid, gmean, [obs_ref[1, n] for n in range(4)], members)
@@ -564,22 +553,20 @@
         return pltpu.make_async_copy(held.at[v], anom_ref.at[v], out_sem.at[0])
 
     def one_field(v, carry):
-        total, before = gather(held_in[v], sources_of(inner, members, taps))
-        block = part_ref[v] - total
+        block, before = gather(held_in[v], sources_of(inner, members, taps), part_ref[v])
         near = sources_of(shifted, members, around(scale, cells))
-        total, mean = gather(block, [*near, (held[fields], *center)])
-        held[v] = block - total
+        held[v], mean = gather(block, [*near, (held[fields], *center)], block)
         mean_ref[v] = fmean_ref[pl.ds(v, 1), :] + before + mean
         save(v).start()
         return carry
 
     lax.fori_loop(0, fields, one_field, 0)
     near = sources_of(shifted, members, around(scale, cells))
-    total, mean = gather(block, [*near, (block, *center)])
+    rest, mean = gather(block, [*near, (block, *center)], block)
     mean_ref[fields] = gmean[:, :cells] + mean
     means = pltpu.make_async_copy(mean_ref, mean_out, out_sem.at[1])
     means.start()
-    held[fields] = block - total
+    held[fields] = rest
     save(fields).start()
     means.wait()
     pltpu.make_async_copy(held, anom_ref, out_sem.at[0]).wait()

time: 18 us -> 17.9 us (level)
  no operation moved by 1% of the time
where the time goes in v6:
time: 17.9 us; the launch traced here: 17.7 us
  Pallas kernels  17.1 us (96%)
  between operations  0.64 us (4%)
    pallas_call x1, Pallas kernels, local(): pl.pallas_call(exchange_kernel, out_shape=results, in_specs=[anywhere] *...  14.4 us
    pallas_call x1, Pallas kernels, local(): pl.pallas_call(analysis_kernel, out_shape=(jax.ShapeDtypeStruct((fields +...  2.69 us

profile of v6, /device:TPU:3, one launch (start us, length us, event | category | flops | bytes accessed | tf_op | source)
XLA Modules:
  0.0 17.7 jit_solution(16246078090853663481)
XLA Ops:
  0.6 14.4 %exchange.1 = (f32[80,128]{1,0:T(8,128)S(1)}, f32[128,128]{1,0:T(8,128)S(1)}, f32[2,4,32,256]{3,2,1,0:T(8,128)S(1)}, f32[12,80,128]{2,1,0:T(8,128)S(1)}, f32[13,...) custom-call(s32[1,4]{1,0:T(1,128)} %bitcast.20, ...), custom_call_target="tpu_custom_call" | custom-call | tf_op jit(solution)/shard_map/exchange/pallas_call | solution.py:595
  15.0 2.7 %analysis.1 = (f32[13,1,128]{2,1,0:T(1,128)}, f32[13,80,128]{2,1,0:T(8,128)}) custom-call(f32[80,128]{1,0:T(8,128)S(1)} %get-tuple-element.12.own_ref, f32[128,128]{1,0:T(8,128)S(1)} %get-tuple-element.13.halo_ref, f32[2,4,32,256]{3,2,1,0:T(8,128)S(1)} %get-tuple-element.14.obs_ref, f32[12,80,128]{2,1,0:T(8,128)S(1)} %get-tuple-element.15.held_in, ...), custom_call_target="tpu_custom_call" | custom-call | tf_op jit(solution)/shard_map/analysis/pallas_call | solution.py:630

commit v7 on v6

--- a/solution.py
+++ b/solution.py
@@ -274,10 +274,10 @@
     start(has_y(-outer), [ocean(0, members, 4, ocn.at[4 + outer], 1, inside, 0, -outer)])
 
     def relay(p, dx):
-        return piece(p, 4 + outer, late.at[int(dx < 0)], 4 + (dx > 0), inside + 1, dx, 0)
+        return piece(p, 4 + outer, late.at[int(dx < 0)], 4 + (dx > 0), inside + 1 + (dx < 0), dx, 0)
 
     def forward(p, dx):
-        return piece(p, 4 + 3 * dx, late.at[int(dx > 0)], 6 + (dx > 0), inside + 1, 0, outer)
+        return piece(p, 4 + 3 * dx, late.at[int(dx > 0)], 6 + (dx > 0), inside + 1 + (dx > 0), 0, outer)
 
     def hand(p, dx):
         return piece(p, 4 + 3 * dx, ocn.at[4 + 3 * dx + outer], 8 + (dx > 0), inside, 0, -outer)
@@ -452,16 +452,15 @@
         position = (source // ny - gx + 1) * 3 + (source % ny - gy + 1)
         places.append(jnp.clip(position, 0, 8))
         total += jnp.dot(ocn[places[k]], wts[k], preferred_element_type=jnp.float32)
-    for n in range(1, 3):
-
-        @pl.when((beside_x == n) & has_y(outer))
-        def _():
-            whole(n, inside + 1, 0, outer)
-
     for dx in (-1, 1):
         match = depth
         for k in range(depth):
             match = jnp.where(places[k] == 4 + 3 * dx + outer, k, match)
+
+        @pl.when(has_x(dx) & has_y(outer))
+        def _():
+            whole(1, inside + 1 + (dx > 0), 0, outer)
+
         total += jnp.dot(late[int(dx > 0)], wts[match], preferred_element_type=jnp.float32)
     own_ref[...] = total
     width = strip_ref.shape[0]
@@ -609,7 +608,7 @@
             pltpu.VMEM((members + 8, 8 * cells), jnp.float32),
             pltpu.SemaphoreType.DMA((7,)),
             pltpu.SemaphoreType.DMA((1,)),
-            pltpu.SemaphoreType.DMA((3 * (members // PIECE) + 2,)),
+            pltpu.SemaphoreType.DMA((3 * (members // PIECE) + 3,)),
             pltpu.SemaphoreType.DMA((2,)),
         ],
         compiler_params=pltpu.CompilerParams(

time: 17.9 us -> 17.8 us (level)
  no operation moved by 1% of the time
where the time goes in v7:
time: 17.8 us; the launch traced here: 17.7 us
  Pallas kernels  17 us (96%)
  between operations  0.64 us (4%)
    pallas_call x1, Pallas kernels, local(): pl.pallas_call(exchange_kernel, out_shape=results, in_specs=[anywhere] *...  14.3 us
    pallas_call x1, Pallas kernels, local(): pl.pallas_call(analysis_kernel, out_shape=(jax.ShapeDtypeStruct((fields +...  2.7 us

profile of v7, /device:TPU:3, one launch (start us, length us, event | category | flops | bytes accessed | tf_op | source)
XLA Modules:
  0.0 17.7 jit_solution(686995658197082524)
XLA Ops:
  0.6 14.3 %exchange.1 = (f32[80,128]{1,0:T(8,128)S(1)}, f32[128,128]{1,0:T(8,128)S(1)}, f32[2,4,32,256]{3,2,1,0:T(8,128)S(1)}, f32[12,80,128]{2,1,0:T(8,128)S(1)}, f32[13,...) custom-call(s32[1,4]{1,0:T(1,128)} %bitcast.20, ...), custom_call_target="tpu_custom_call" | custom-call | tf_op jit(solution)/shard_map/exchange/pallas_call | solution.py:594
  15.0 2.7 %analysis.1 = (f32[13,1,128]{2,1,0:T(1,128)}, f32[13,80,128]{2,1,0:T(8,128)}) custom-call(f32[80,128]{1,0:T(8,128)S(1)} %get-tuple-element.12.own_ref, f32[128,128]{1,0:T(8,128)S(1)} %get-tuple-element.13.halo_ref, f32[2,4,32,256]{3,2,1,0:T(8,128)S(1)} %get-tuple-element.14.obs_ref, f32[12,80,128]{2,1,0:T(8,128)S(1)} %get-tuple-element.15.held_in, ...), custom_call_target="tpu_custom_call" | custom-call | tf_op jit(solution)/shard_map/analysis/pallas_call | solution.py:629

commit v8 on v7

--- a/solution.py
+++ b/solution.py
@@ -260,7 +260,7 @@
     beside, inside = 2 * count, 3 * count
 
     mine = lax.rem(gy, 8)
-    yields = (mine == 2) | (mine == 5)
+    yields = mine == 2
     to_outer = [piece(p, 4, ocn.at[4 - outer], 0, beside + p, 0, outer) for p in order]
     start(has_y(outer) & jnp.logical_not(yields), to_outer)
     for dx in (-1, 1):

time: 17.8 us -> 17.8 us (level)
  no operation moved by 1% of the time
where the time goes in v8:
time: 17.8 us; the launch traced here: 17.7 us
  Pallas kernels  17 us (96%)
  between operations  0.64 us (4%)
    pallas_call x1, Pallas kernels, local(): pl.pallas_call(exchange_kernel, out_shape=results, in_specs=[anywhere] *...  14.3 us
    pallas_call x1, Pallas kernels, local(): pl.pallas_call(analysis_kernel, out_shape=(jax.ShapeDtypeStruct((fields +...  2.7 us

profile of v8, /device:TPU:3, one launch (start us, length us, event | category | flops | bytes accessed | tf_op | source)
XLA Modules:
  0.0 17.7 jit_solution(3718325961804408841)
XLA Ops:
  0.6 14.3 %exchange.1 = (f32[80,128]{1,0:T(8,128)S(1)}, f32[128,128]{1,0:T(8,128)S(1)}, f32[2,4,32,256]{3,2,1,0:T(8,128)S(1)}, f32[12,80,128]{2,1,0:T(8,128)S(1)}, f32[13,...) custom-call(s32[1,4]{1,0:T(1,128)} %bitcast.20, ...), custom_call_target="tpu_custom_call" | custom-call | tf_op jit(solution)/shard_map/exchange/pallas_call | solution.py:594
  15.0 2.7 %analysis.1 = (f32[13,1,128]{2,1,0:T(1,128)}, f32[13,80,128]{2,1,0:T(8,128)}) custom-call(f32[80,128]{1,0:T(8,128)S(1)} %get-tuple-element.12.own_ref, f32[128,128]{1,0:T(8,128)S(1)} %get-tuple-element.13.halo_ref, f32[2,4,32,256]{3,2,1,0:T(8,128)S(1)} %get-tuple-element.14.obs_ref, f32[12,80,128]{2,1,0:T(8,128)S(1)} %get-tuple-element.15.held_in, ...), custom_call_target="tpu_custom_call" | custom-call | tf_op jit(solution)/shard_map/analysis/pallas_call | solution.py:629
